TPU v7x, 256 devices: a whole 4x4x8 slice. The times are simulated.
256 devices in a mesh: seq: 128 (over z, x_hi, y, core), head: 2 (over x_lo).
Axes of the slice: x: 4 (x_hi: 2, x_lo: 2; x = x_hi * 2 + x_lo), y: 4, z: 8, core: 2. Of those that a mesh axis runs over, the one named last changes fastest.
Arguments:
- queries: bfloat16 [32768, 512], P('seq', 'head'), may hold values from -4 to 4
- values: bfloat16 [32768, 512], P('seq', 'head'), may hold values from -6 to 6
- scales: float32 [32768, 8], P('seq', 'head'), may hold values from 2 to 20
- block_reach: int32 [128], P('seq'), may hold values from 1 to 4
- out_weight: bfloat16 [512, 1024], P('head'), may hold values from -0.25 to 0.25
- out_grad: bfloat16 [32768, 512], P('seq', 'head'), may hold values from -6 to 6
Outputs:
- mixed: bfloat16 [32768, 1024], P(('seq', 'head'))
- value_grad: bfloat16 [32768, 512], P('seq', 'head')
All inputs are finite; a program needn't handle non-finite values.
Results may differ from a plain program's by a relative error of at most 0.0015.
The roundings to bfloat16 on the way count: a program that leaves them out, or rounds other values in their place, can miss the bound.
Values may be sent and summed in bfloat16 or wider, within the bound.
A program may use at most 64 MiB of HBM per device.

v0:
```python
import jax
import jax.numpy as jnp
from jax import lax
from jax.sharding import PartitionSpec as P

HD = 64
WINDOW = 4


NEGATIVE = -1e30


def from_behind(value, axis, steps):
    count = lax.axis_size(axis)
    initial, last = (max(0, -steps), min(count, count - steps))
    return lax.ppermute(value, axis, [(source, source + steps) for source in range(initial, last)])


def in_blocks(array, dim, peers):
    dims = array.shape
    blocks = array.reshape(*dims[:dim], peers, dims[dim] // peers, *dims[dim + 1 :])
    return jnp.moveaxis(blocks, dim, 0)


def sum_at_owner(array, axis, dim):
    peers = lax.axis_size(axis)
    blocks = lax.all_to_all(in_blocks(array, dim, peers), axis, 0, 0, tiled=True)
    return jnp.sum(blocks, axis=0)


def unit_keys(queries, scales):
    as_float = queries.astype(jnp.float32).reshape(queries.shape[0], scales.shape[1], HD)
    direction = as_float * lax.rsqrt(jnp.sum(as_float * as_float, axis=-1, keepdims=True) + 1e-06)
    return (direction * scales[:, :, None]).astype(jnp.bfloat16)


def tile_scores(row_keys, column_keys):
    return jnp.einsum("ihd,jhd->hij", row_keys, column_keys, preferred_element_type=jnp.float32)


def row_part(scores, allowed, column_values):
    tile_top = jnp.max(scores, axis=2)
    exponent = jnp.exp(scores - tile_top[:, :, None]) * allowed
    numerator = jnp.einsum(
        "hij,jhd->ihd",
        exponent.astype(jnp.bfloat16),
        column_values,
        preferred_element_type=jnp.float32,
    )
    return (jnp.where(allowed > 0, tile_top, NEGATIVE), jnp.sum(exponent, axis=2), numerator)


def column_part(scores, allowed, row_values):
    tile_top = jnp.max(scores, axis=1)
    exponent = jnp.exp(scores - tile_top[:, None, :]) * allowed
    numerator = jnp.einsum(
        "hij,ihd->jhd",
        exponent.astype(jnp.bfloat16),
        row_values,
        preferred_element_type=jnp.float32,
    )
    return (jnp.where(allowed > 0, tile_top, NEGATIVE), jnp.sum(exponent, axis=1), numerator)


def merge_stats(former, latter):
    top_one = jnp.where(former[1] > 0, former[0], NEGATIVE)
    top_two = jnp.where(latter[1] > 0, latter[0], NEGATIVE)
    maximum = jnp.maximum(top_one, top_two)
    factor_one = jnp.exp(top_one - maximum)
    factor_two = jnp.exp(top_two - maximum)
    summed = factor_one * former[1] + factor_two * latter[1]
    numerator = former[2] * factor_one.T[:, :, None] + latter[2] * factor_two.T[:, :, None]
    return (maximum, summed, numerator)


def packed(stats):
    return (stats[0], stats[1], stats[2].reshape(stats[2].shape[0], -1))


def unpacked(stats, head_count):
    return (stats[0], stats[1], stats[2].reshape(stats[2].shape[0], head_count, -1))


def shards(queries, values, scales, block_reach, out_weight, out_grad):
    length = queries.shape[0]
    head_count = scales.shape[1]
    key_rows = unit_keys(queries, scales)
    key_flat = key_rows.reshape(length, head_count * HD)
    value_rows = values.reshape(length, head_count, HD)
    diagonal = jnp.eye(length, dtype=bool)
    self_scores = jnp.where(diagonal[None], NEGATIVE, tile_scores(key_rows, key_rows))
    running = row_part(self_scores, 1.0, value_rows)
    partials = []
    visitors = []
    moving = (key_flat, values, block_reach)
    for distance in range(1, WINDOW + 1):
        moving = from_behind((moving[0], moving[1], moving[2]), "seq", 1)
        far_keys = moving[0].reshape(length, head_count, HD)
        far_values = moving[1].reshape(length, head_count, HD)
        allowed = (distance <= jnp.minimum(block_reach[0], moving[2][0])).astype(jnp.float32)
        scores = tile_scores(key_rows, far_keys)
        running = merge_stats(running, row_part(scores, allowed, far_values))
        partials.append(column_part(scores, allowed, value_rows))
        visitors.append((far_keys, allowed))
    for distance in range(1, WINDOW + 1):
        returned = from_behind(packed(partials[distance - 1]), "seq", -distance)
        running = merge_stats(running, unpacked(returned, head_count))
    row_top, totals, numerator = running
    attended = (
        (numerator / totals.T[:, :, None]).astype(jnp.bfloat16).reshape(length, head_count * HD)
    )
    mixed = sum_at_owner(
        jnp.dot(attended, out_weight, preferred_element_type=jnp.float32), "head", 0
    ).astype(jnp.bfloat16)
    grad_rows = out_grad.reshape(length, head_count, HD)
    own_weights = (jnp.exp(self_scores - row_top[:, :, None]) / totals[:, :, None]).astype(
        jnp.bfloat16
    )
    grad_here = jnp.einsum(
        "hij,ihd->jhd", own_weights, grad_rows, preferred_element_type=jnp.float32
    )
    returns = []
    travel_grad = out_grad
    travel_stats = (row_top, totals)
    for distance in range(1, WINDOW + 1):
        travel_grad = from_behind(travel_grad, "seq", 1)
        travel_stats = from_behind((travel_stats[0], travel_stats[1]), "seq", 1)
        far_keys, allowed = visitors[distance - 1]
        far_grads = travel_grad.reshape(length, head_count, HD)
        far_top = travel_stats[0]
        far_total = travel_stats[1]
        scores = tile_scores(key_rows, far_keys)
        near_weights = jnp.where(
            allowed > 0, jnp.exp(scores - row_top[:, :, None]) / totals[:, :, None], 0.0
        ).astype(jnp.bfloat16)
        returns.append(
            jnp.einsum("hij,ihd->jhd", near_weights, grad_rows, preferred_element_type=jnp.float32)
        )
        far_weights = jnp.where(
            allowed > 0, jnp.exp(scores - far_top[:, None, :]) / far_total[:, None, :], 0.0
        ).astype(jnp.bfloat16)
        grad_here = grad_here + jnp.einsum(
            "hij,jhd->ihd", far_weights, far_grads, preferred_element_type=jnp.float32
        )
    for distance in range(1, WINDOW + 1):
        returned = from_behind(returns[distance - 1].reshape(length, -1), "seq", -distance)
        grad_here = grad_here + returned.reshape(length, head_count, HD)
    value_grad = grad_here.astype(jnp.bfloat16).reshape(length, head_count * HD)
    return (mixed, value_grad)


def solution(mesh):
    return jax.shard_map(
        shards,
        mesh=mesh,
        in_specs=(
            P("seq", "head"),
            P("seq", "head"),
            P("seq", "head"),
            P("seq"),
            P("head", None),
            P("seq", "head"),
        ),
        out_specs=(P(("seq", "head"), None), P("seq", "head")),
        check_vma=False,
    )
```

profile of v0, /device:TPU:166, one launch (start us, length us, event | category | flops | bytes accessed | tf_op | source)
XLA Modules:
  0.0 258.8 jit_solution(15893186239708439859)
XLA Ops:
  4.5 3.6 %collective-permute-start.1 = (s32[1]{0:T(128)}, s32[1]{0:T(128)}, u32[]{:S(2)}, u32[]{:S(2)}) collective-permute-start(s32[1]{0:T(128)} %param.9), channel_id=1, source_target_pairs={{0,2},{2,4},{4,6},{6,8},{8,10},{10,12},{12,14},{14,16},{16,18},{18... | collective-permute-start | bytes 20 | tf_op jit(solution)/shard_map/ppermute | solution.py:16
  10.1 3.6 %collective-permute-start.26 = (bf16[256,256]{1,0:T(8,128)(2,1)S(1)}, bf16[256,256]{1,0:T(8,128)(2,1)}, u32[]{:S(2)}, u32[]{:S(2)}) collective-permute-start(bf16[256,256]{1,0:T(8,128)(2,1)S(1)} %copy-done.15), channel_id=1, source_target_pairs={{0,2},{2,4},{4,6},{6,8},{8,10},{10,12},{12,14},{14,16},{16,18},{18... | collective-permute-start | bytes 393224 | tf_op jit(solution)/shard_map/ppermute | solution.py:16
  19.4 6.7 %collective-permute-done.4 = s32[1]{0:T(128)} collective-permute-done((s32[1]{0:T(128)}, s32[1]{0:T(128)}, u32[]{:S(2)}, u32[]{:S(2)}) %collective-permute-start.4) | collective-permute-done | bytes 36 | tf_op jit(solution)/shard_map/ppermute | solution.py:16
  28.6 6.7 %collective-permute-done.7 = s32[1]{0:T(128)} collective-permute-done((s32[1]{0:T(128)}, s32[1]{0:T(128)}, u32[]{:S(2)}, u32[]{:S(2)}) %collective-permute-start.7) | collective-permute-done | bytes 36 | tf_op jit(solution)/shard_map/ppermute | solution.py:16
  38.0 6.7 %collective-permute-done.10 = s32[1]{0:T(128)} collective-permute-done((s32[1]{0:T(128)}, s32[1]{0:T(128)}, u32[]{:S(2)}, u32[]{:S(2)}) %collective-permute-start.10) | collective-permute-done | bytes 36 | tf_op jit(solution)/shard_map/ppermute | solution.py:16
  57.3 3.6 %collective-permute-start.5 = (bf16[256,256]{1,0:T(8,128)(2,1)S(1)}, bf16[256,256]{1,0:T(8,128)(2,1)}, u32[]{:S(2)}, u32[]{:S(2)}) collective-permute-start(bf16[256,256]{1,0:T(8,128)(2,1)S(1)} %collective-permute-done.2), channel_id=1, source_target_pairs={{0,2},{2,4},{4,6},{6,8},{8,10},{10,12},{12,14},{14,16},{16,18},{18... | collective-permute-start | bytes 393224 | tf_op jit(solution)/shard_map/ppermute | solution.py:16
  69.0 4.5 %collective-permute-start.16 = (f32[4,256]{1,0:T(4,128)}, f32[4,256]{1,0:T(4,128)}, u32[]{:S(2)}, u32[]{:S(2)}) collective-permute-start(f32[4,256]{1,0:T(4,128)} %broadcast_select_fusion.1), channel_id=1, source_target_pairs={{4,0},{6,2},{8,4},{10,6},{12,8},{14,10},{16,12},{18,14},{20,16},{2... | collective-permute-start | bytes 12296 | tf_op jit(solution)/shard_map/ppermute | solution.py:16
  75.5 4.8 %collective-permute-start.6 = (bf16[256,256]{0,1:T(8,128)(2,1)S(1)}, bf16[256,256]{0,1:T(8,128)(2,1)}, u32[]{:S(2)}, u32[]{:S(2)}) collective-permute-start(bf16[256,256]{0,1:T(8,128)(2,1)S(1)} %collective-permute-done.3), channel_id=1, source_target_pairs={{0,2},{2,4},{4,6},{6,8},{8,10},{10,12},{12,14},{14,16},{16,18},{18... | collective-permute-start | bytes 393224 | tf_op jit(solution)/shard_map/ppermute | solution.py:16
  87.4 2.8 %fusion.124 = (f32[4,256]{1,0:T(4,128)}, f32[4,256]{1,0:T(4,128)S(1)}, f32[4,256,256]{2,1,0:T(8,128)}) fusion(bf16[256,4,64]{0,2,1:T(8,128)(2,1)S(1)} %multiply_convert_fusion, bf16[256,4,64]{0,2,1:T(8,128)(2,1)} %bitcast.19), kind=kOutput, calls=%fused_computation.207 | convolution fusion | flops 34076672 | bytes 1318912 | tf_op jit(solution)/shard_map/ihd,jhd->hij/dot_general | solution.py:38
  90.3 2.6 copy.69
  99.8 6.7 %collective-permute-done.32 = bf16[256,256]{1,0:T(8,128)(2,1)} collective-permute-done((bf16[256,256]{1,0:T(8,128)(2,1)}, bf16[256,256]{1,0:T(8,128)(2,1)}, u32[]{:S(2)}, u32[]{:S(2)}) %collective-permute-start.32) | collective-permute-done | bytes 131104 | tf_op jit(solution)/shard_map/ppermute | solution.py:16
  111.8 4.9 %collective-permute-done.9 = bf16[256,256]{0,1:T(8,128)(2,1)} collective-permute-done((bf16[256,256]{0,1:T(8,128)(2,1)}, bf16[256,256]{0,1:T(8,128)(2,1)}, u32[]{:S(2)}, u32[]{:S(2)}) %collective-permute-start.9) | collective-permute-done | bytes 131104 | tf_op jit(solution)/shard_map/ppermute | solution.py:16
  128.5 14.0 %collective-permute-start.18 = (f32[4,256]{1,0:T(4,128)S(1)}, f32[4,256]{1,0:T(4,128)S(1)}, u32[]{:S(2)}, u32[]{:S(2)}) collective-permute-start(f32[4,256]{1,0:T(4,128)S(1)} %get-tuple-element.10), channel_id=1, source_target_pairs={{6,0},{8,2},{10,4},{12,6},{14,8},{16,10},{18,12},{20,14},{22,16},{... | collective-permute-start | bytes 12296 | tf_op jit(solution)/shard_map/ppermute | solution.py:16
  149.0 4.1 %collective-permute-start.22 = (f32[4,256]{1,0:T(4,128)S(1)}, f32[4,256]{1,0:T(4,128)S(1)}, u32[]{:S(2)}, u32[]{:S(2)}) collective-permute-start(f32[4,256]{1,0:T(4,128)S(1)} %broadcast_select_fusion.3), channel_id=1, source_target_pairs={{8,0},{10,2},{12,4},{14,6},{16,8},{18,10},{20,12},{22,14},{24,16},... | collective-permute-start | bytes 12296 | tf_op jit(solution)/shard_map/ppermute | solution.py:16
  158.0 6.1 %collective-permute-start.17 = (f32[256,256]{0,1:T(8,128)S(1)}, f32[256,256]{0,1:T(8,128)}, u32[]{:S(2)}, u32[]{:S(2)}) collective-permute-start(f32[256,256]{0,1:T(8,128)S(1)} %bitcast.288), channel_id=1, source_target_pairs={{4,0},{6,2},{8,4},{10,6},{12,8},{14,10},{16,12},{18,14},{20,16},{2... | collective-permute-start | bytes 786440 | tf_op jit(solution)/shard_map/ppermute | solution.py:16
  178.3 2.6 %collective-permute-start.28 = (f32[4,256]{1,0:T(4,128)S(1)}, f32[4,256]{1,0:T(4,128)S(1)}, u32[]{:S(2)}, u32[]{:S(2)}) collective-permute-start(f32[4,256]{1,0:T(4,128)S(1)} %collective-permute-done.25), channel_id=1, source_target_pairs={{0,2},{2,4},{4,6},{6,8},{8,10},{10,12},{12,14},{14,16},{16,18},{18... | collective-permute-start | bytes 12296 | tf_op jit(solution)/shard_map/ppermute | solution.py:16
  180.9 2.7 %collective-permute-start.27 = (f32[4,256]{1,0:T(4,128)S(1)}, f32[4,256]{1,0:T(4,128)S(1)}, u32[]{:S(2)}, u32[]{:S(2)}) collective-permute-start(f32[4,256]{1,0:T(4,128)S(1)} %collective-permute-done.24), channel_id=1, source_target_pairs={{0,2},{2,4},{4,6},{6,8},{8,10},{10,12},{12,14},{14,16},{16,18},{18... | collective-permute-start | bytes 12296 | tf_op jit(solution)/shard_map/ppermute | solution.py:16
  186.8 15.7 %collective-permute-start.23 = (f32[256,256]{0,1:T(8,128)S(1)}, f32[256,256]{0,1:T(8,128)S(1)}, u32[]{:S(2)}, u32[]{:S(2)}) collective-permute-start(f32[256,256]{0,1:T(8,128)S(1)} %bitcast.289), channel_id=1, source_target_pairs={{8,0},{10,2},{12,4},{14,6},{16,8},{18,10},{20,12},{22,14},{24,16},... | collective-permute-start | bytes 786440 | tf_op jit(solution)/shard_map/ppermute | solution.py:16
  205.9 10.0 %collective-permute-start.39 = (f32[256,256]{0,1:T(8,128)}, f32[256,256]{0,1:T(8,128)}, u32[]{:S(2)}, u32[]{:S(2)}) collective-permute-start(f32[256,256]{0,1:T(8,128)} %bitcast.68), channel_id=1, source_target_pairs={{8,0},{10,2},{12,4},{14,6},{16,8},{18,10},{20,12},{22,14},{24,16},... | collective-permute-start | bytes 786440 | tf_op jit(solution)/shard_map/ppermute | solution.py:16
  216.0 4.2 %collective-permute-start.38 = (f32[256,256]{0,1:T(8,128)}, f32[256,256]{0,1:T(8,128)}, u32[]{:S(2)}, u32[]{:S(2)}) collective-permute-start(f32[256,256]{0,1:T(8,128)} %bitcast.65), channel_id=1, source_target_pairs={{6,0},{8,2},{10,4},{12,6},{14,8},{16,10},{18,12},{20,14},{22,16},{... | collective-permute-start | bytes 786440 | tf_op jit(solution)/shard_map/ppermute | solution.py:16
  220.2 6.8 %collective-permute-start.37 = (f32[256,256]{0,1:T(8,128)}, f32[256,256]{0,1:T(8,128)}, u32[]{:S(2)}, u32[]{:S(2)}) collective-permute-start(f32[256,256]{0,1:T(8,128)} %bitcast.62), channel_id=1, source_target_pairs={{4,0},{6,2},{8,4},{10,6},{12,8},{14,10},{16,12},{18,14},{20,16},{2... | collective-permute-start | bytes 786440 | tf_op jit(solution)/shard_map/ppermute | solution.py:16
  234.5 3.7 %all-to-all-start = ((f32[2,128,1024]{2,1,0:T(8,128)}), f32[2,128,1024]{2,1,0:T(8,128)S(1)}, u32[]{:S(2)}, u32[]{:S(2)}) async-start(f32[2,128,1024]{2,1,0:T(8,128)} %fusion.59), calls=%async_computation | async-start | bytes 2097152 | tf_op jit(solution)/shard_map/all_to_all | solution.py:27
  238.2 7.5 %collective-permute-start.36 = (f32[256,256]{0,1:T(8,128)S(1)}, f32[256,256]{0,1:T(8,128)S(1)}, u32[]{:S(2)}, u32[]{:S(2)}) collective-permute-start(f32[256,256]{0,1:T(8,128)S(1)} %bitcast.304), channel_id=1, source_target_pairs={{2,0},{4,2},{6,4},{8,6},{10,8},{12,10},{14,12},{16,14},{18,16},{20... | collective-permute-start | bytes 786440 | tf_op jit(solution)/shard_map/ppermute | solution.py:16
  249.2 6.4 %collective-permute-done.33 = f32[4,256]{1,0:T(4,128)S(1)} collective-permute-done((f32[4,256]{1,0:T(4,128)S(1)}, f32[4,256]{1,0:T(4,128)S(1)}, u32[]{:S(2)}, u32[]{:S(2)}) %collective-permute-start.33) | collective-permute-done | bytes 4128 | tf_op jit(solution)/shard_map/ppermute | solution.py:16
  (206 shorter events, 113.0 us)
Async XLA Ops:
  2.5 42.8 %collective-permute-start = (bf16[256,256]{0,1:T(8,128)(2,1)S(1)}, bf16[256,256]{0,1:T(8,128)(2,1)S(1)}, u32[]{:S(2)}, u32[]{:S(2)}) collective-permute-start(bf16[256,256]{0,1:T(8,128)(2,1)S(1)} %fusion.90), channel_id=1, source_target_pairs={{0,2},{2,4},{4,6},{6,8},{8,10},{10,12},{12,14},{14,16},{16,18},{18... | collective-permute-start | bytes 393224 | tf_op jit(solution)/shard_map/ppermute | solution.py:16
  8.2 46.6 %collective-permute-start.2 = (bf16[256,256]{1,0:T(8,128)(2,1)S(1)}, bf16[256,256]{1,0:T(8,128)(2,1)S(1)}, u32[]{:S(2)}, u32[]{:S(2)}) collective-permute-start(bf16[256,256]{1,0:T(8,128)(2,1)S(1)} %copy-done.14), channel_id=1, source_target_pairs={{0,2},{2,4},{4,6},{6,8},{8,10},{10,12},{12,14},{14,16},{16,18},{18... | collective-permute-start | bytes 393224 | tf_op jit(solution)/shard_map/ppermute | solution.py:16
  10.1 47.2 %collective-permute-start.26 = (bf16[256,256]{1,0:T(8,128)(2,1)S(1)}, bf16[256,256]{1,0:T(8,128)(2,1)}, u32[]{:S(2)}, u32[]{:S(2)}) collective-permute-start(bf16[256,256]{1,0:T(8,128)(2,1)S(1)} %copy-done.15), channel_id=1, source_target_pairs={{0,2},{2,4},{4,6},{6,8},{8,10},{10,12},{12,14},{14,16},{16,18},{18... | collective-permute-start | bytes 393224 | tf_op jit(solution)/shard_map/ppermute | solution.py:16
  47.4 158.6 %collective-permute-start.14 = (f32[256,256]{0,1:T(8,128)S(1)}, f32[256,256]{0,1:T(8,128)}, u32[]{:S(2)}, u32[]{:S(2)}) collective-permute-start(f32[256,256]{0,1:T(8,128)S(1)} %bitcast.287), channel_id=1, source_target_pairs={{2,0},{4,2},{6,4},{8,6},{10,8},{12,10},{14,12},{16,14},{18,16},{20... | collective-permute-start | bytes 786440 | tf_op jit(solution)/shard_map/ppermute | solution.py:16
  49.9 76.6 %collective-permute-start.13 = (f32[4,256]{1,0:T(4,128)}, f32[4,256]{1,0:T(4,128)}, u32[]{:S(2)}, u32[]{:S(2)}) collective-permute-start(f32[4,256]{1,0:T(4,128)} %broadcast_select_fusion.2), channel_id=1, source_target_pairs={{2,0},{4,2},{6,4},{8,6},{10,8},{12,10},{14,12},{16,14},{18,16},{20... | collective-permute-start | bytes 12296 | tf_op jit(solution)/shard_map/ppermute | solution.py:16
  52.9 75.6 %collective-permute-start.12 = (f32[4,256]{1,0:T(4,128)}, f32[4,256]{1,0:T(4,128)}, u32[]{:S(2)}, u32[]{:S(2)}) collective-permute-start(f32[4,256]{1,0:T(4,128)} %get-tuple-element.6), channel_id=1, source_target_pairs={{2,0},{4,2},{6,4},{8,6},{10,8},{12,10},{14,12},{16,14},{18,16},{20... | collective-permute-start | bytes 12296 | tf_op jit(solution)/shard_map/ppermute | solution.py:16
  69.0 74.8 %collective-permute-start.16 = (f32[4,256]{1,0:T(4,128)}, f32[4,256]{1,0:T(4,128)}, u32[]{:S(2)}, u32[]{:S(2)}) collective-permute-start(f32[4,256]{1,0:T(4,128)} %broadcast_select_fusion.1), channel_id=1, source_target_pairs={{4,0},{6,2},{8,4},{10,6},{12,8},{14,10},{16,12},{18,14},{20,16},{2... | collective-permute-start | bytes 12296 | tf_op jit(solution)/shard_map/ppermute | solution.py:16
  116.7 29.1 %collective-permute-start.15 = (f32[4,256]{1,0:T(4,128)S(1)}, f32[4,256]{1,0:T(4,128)S(1)}, u32[]{:S(2)}, u32[]{:S(2)}) collective-permute-start(f32[4,256]{1,0:T(4,128)S(1)} %copy-done.34), channel_id=1, source_target_pairs={{4,0},{6,2},{8,4},{10,6},{12,8},{14,10},{16,12},{18,14},{20,16},{2... | collective-permute-start | bytes 12296 | tf_op jit(solution)/shard_map/ppermute | solution.py:16
  126.5 22.5 %collective-permute-start.19 = (f32[4,256]{1,0:T(4,128)S(1)}, f32[4,256]{1,0:T(4,128)S(1)}, u32[]{:S(2)}, u32[]{:S(2)}) collective-permute-start(f32[4,256]{1,0:T(4,128)S(1)} %copy-done.37), channel_id=1, source_target_pairs={{6,0},{8,2},{10,4},{12,6},{14,8},{16,10},{18,12},{20,14},{22,16},{... | collective-permute-start | bytes 12296 | tf_op jit(solution)/shard_map/ppermute | solution.py:16
  128.5 24.6 %collective-permute-start.18 = (f32[4,256]{1,0:T(4,128)S(1)}, f32[4,256]{1,0:T(4,128)S(1)}, u32[]{:S(2)}, u32[]{:S(2)}) collective-permute-start(f32[4,256]{1,0:T(4,128)S(1)} %get-tuple-element.10), channel_id=1, source_target_pairs={{6,0},{8,2},{10,4},{12,6},{14,8},{16,10},{18,12},{20,14},{22,16},{... | collective-permute-start | bytes 12296 | tf_op jit(solution)/shard_map/ppermute | solution.py:16
  145.8 19.1 %collective-permute-start.35 = (bf16[256,256]{1,0:T(8,128)(2,1)}, bf16[256,256]{1,0:T(8,128)(2,1)S(1)}, u32[]{:S(2)}, u32[]{:S(2)}) collective-permute-start(bf16[256,256]{1,0:T(8,128)(2,1)} %collective-permute-done.32), channel_id=1, source_target_pairs={{0,2},{2,4},{4,6},{6,8},{8,10},{10,12},{12,14},{14,16},{16,18},{18... | collective-permute-start | bytes 393224 | tf_op jit(solution)/shard_map/ppermute | solution.py:16
  149.0 18.7 %collective-permute-start.22 = (f32[4,256]{1,0:T(4,128)S(1)}, f32[4,256]{1,0:T(4,128)S(1)}, u32[]{:S(2)}, u32[]{:S(2)}) collective-permute-start(f32[4,256]{1,0:T(4,128)S(1)} %broadcast_select_fusion.3), channel_id=1, source_target_pairs={{8,0},{10,2},{12,4},{14,6},{16,8},{18,10},{20,12},{22,14},{24,16},... | collective-permute-start | bytes 12296 | tf_op jit(solution)/shard_map/ppermute | solution.py:16
  153.1 14.6 %collective-permute-start.21 = (f32[4,256]{1,0:T(4,128)}, f32[4,256]{1,0:T(4,128)S(1)}, u32[]{:S(2)}, u32[]{:S(2)}) collective-permute-start(f32[4,256]{1,0:T(4,128)} %get-tuple-element.12), channel_id=1, source_target_pairs={{8,0},{10,2},{12,4},{14,6},{16,8},{18,10},{20,12},{22,14},{24,16},... | collective-permute-start | bytes 12296 | tf_op jit(solution)/shard_map/ppermute | solution.py:16
  158.0 58.0 %collective-permute-start.17 = (f32[256,256]{0,1:T(8,128)S(1)}, f32[256,256]{0,1:T(8,128)}, u32[]{:S(2)}, u32[]{:S(2)}) collective-permute-start(f32[256,256]{0,1:T(8,128)S(1)} %bitcast.288), channel_id=1, source_target_pairs={{4,0},{6,2},{8,4},{10,6},{12,8},{14,10},{16,12},{18,14},{20,16},{2... | collective-permute-start | bytes 786440 | tf_op jit(solution)/shard_map/ppermute | solution.py:16
  164.8 62.1 %collective-permute-start.20 = (f32[256,256]{0,1:T(8,128)}, f32[256,256]{0,1:T(8,128)}, u32[]{:S(2)}, u32[]{:S(2)}) collective-permute-start(f32[256,256]{0,1:T(8,128)} %bitcast.42), channel_id=1, source_target_pairs={{6,0},{8,2},{10,4},{12,6},{14,8},{16,10},{18,12},{20,14},{22,16},{... | collective-permute-start | bytes 786440 | tf_op jit(solution)/shard_map/ppermute | solution.py:16
  180.9 21.6 %collective-permute-start.27 = (f32[4,256]{1,0:T(4,128)S(1)}, f32[4,256]{1,0:T(4,128)S(1)}, u32[]{:S(2)}, u32[]{:S(2)}) collective-permute-start(f32[4,256]{1,0:T(4,128)S(1)} %collective-permute-done.24), channel_id=1, source_target_pairs={{0,2},{2,4},{4,6},{6,8},{8,10},{10,12},{12,14},{14,16},{16,18},{18... | collective-permute-start | bytes 12296 | tf_op jit(solution)/shard_map/ppermute | solution.py:16
  186.8 42.1 %collective-permute-start.23 = (f32[256,256]{0,1:T(8,128)S(1)}, f32[256,256]{0,1:T(8,128)S(1)}, u32[]{:S(2)}, u32[]{:S(2)}) collective-permute-start(f32[256,256]{0,1:T(8,128)S(1)} %bitcast.289), channel_id=1, source_target_pairs={{8,0},{10,2},{12,4},{14,6},{16,8},{18,10},{20,12},{22,14},{24,16},... | collective-permute-start | bytes 786440 | tf_op jit(solution)/shard_map/ppermute | solution.py:16
  202.5 17.6 %collective-permute-start.31 = (f32[4,256]{1,0:T(4,128)S(1)}, f32[4,256]{1,0:T(4,128)S(1)}, u32[]{:S(2)}, u32[]{:S(2)}) collective-permute-start(f32[4,256]{1,0:T(4,128)S(1)} %collective-permute-done.28), channel_id=1, source_target_pairs={{0,2},{2,4},{4,6},{6,8},{8,10},{10,12},{12,14},{14,16},{16,18},{18... | collective-permute-start | bytes 12296 | tf_op jit(solution)/shard_map/ppermute | solution.py:16
  205.9 49.7 %collective-permute-start.39 = (f32[256,256]{0,1:T(8,128)}, f32[256,256]{0,1:T(8,128)}, u32[]{:S(2)}, u32[]{:S(2)}) collective-permute-start(f32[256,256]{0,1:T(8,128)} %bitcast.68), channel_id=1, source_target_pairs={{8,0},{10,2},{12,4},{14,6},{16,8},{18,10},{20,12},{22,14},{24,16},... | collective-permute-start | bytes 786440 | tf_op jit(solution)/shard_map/ppermute | solution.py:16
  216.0 39.6 %collective-permute-start.38 = (f32[256,256]{0,1:T(8,128)}, f32[256,256]{0,1:T(8,128)}, u32[]{:S(2)}, u32[]{:S(2)}) collective-permute-start(f32[256,256]{0,1:T(8,128)} %bitcast.65), channel_id=1, source_target_pairs={{6,0},{8,2},{10,4},{12,6},{14,8},{16,10},{18,12},{20,14},{22,16},{... | collective-permute-start | bytes 786440 | tf_op jit(solution)/shard_map/ppermute | solution.py:16
  220.2 35.4 %collective-permute-start.37 = (f32[256,256]{0,1:T(8,128)}, f32[256,256]{0,1:T(8,128)}, u32[]{:S(2)}, u32[]{:S(2)}) collective-permute-start(f32[256,256]{0,1:T(8,128)} %bitcast.62), channel_id=1, source_target_pairs={{4,0},{6,2},{8,4},{10,6},{12,8},{14,10},{16,12},{18,14},{20,16},{2... | collective-permute-start | bytes 786440 | tf_op jit(solution)/shard_map/ppermute | solution.py:16
  228.9 16.8 %collective-permute-start.34 = (f32[4,256]{1,0:T(4,128)S(1)}, f32[4,256]{1,0:T(4,128)S(1)}, u32[]{:S(2)}, u32[]{:S(2)}) collective-permute-start(f32[4,256]{1,0:T(4,128)S(1)} %collective-permute-done.31), channel_id=1, source_target_pairs={{0,2},{2,4},{4,6},{6,8},{8,10},{10,12},{12,14},{14,16},{16,18},{18... | collective-permute-start | bytes 12296 | tf_op jit(solution)/shard_map/ppermute | solution.py:16
  234.5 23.5 %all-to-all-start = ((f32[2,128,1024]{2,1,0:T(8,128)}), f32[2,128,1024]{2,1,0:T(8,128)S(1)}, u32[]{:S(2)}, u32[]{:S(2)}) async-start(f32[2,128,1024]{2,1,0:T(8,128)} %fusion.59), calls=%async_computation | async-start | bytes 2097152 | tf_op jit(solution)/shard_map/all_to_all | solution.py:27
  238.2 17.4 %collective-permute-start.36 = (f32[256,256]{0,1:T(8,128)S(1)}, f32[256,256]{0,1:T(8,128)S(1)}, u32[]{:S(2)}, u32[]{:S(2)}) collective-permute-start(f32[256,256]{0,1:T(8,128)S(1)} %bitcast.304), channel_id=1, source_target_pairs={{2,0},{4,2},{6,4},{8,6},{10,8},{12,10},{14,12},{16,14},{18,16},{20... | collective-permute-start | bytes 786440 | tf_op jit(solution)/shard_map/ppermute | solution.py:16
  (58 other events, 770.2 us)
where the time goes:
time: 261 us; the launch traced here: 259 us
  starting transfers between devices  147 us (56%)
  waiting for transfers between devices  45.9 us (18%)
  local copies, waits for them, and re-layouts  24.9 us (10%)
  matrix products  23.2 us (9%)
  other arithmetic  13.1 us (5%)
  between operations  4.74 us (2%)
    ppermute x40, starting transfers between devices, from_behind(): lax.ppermute(value, axis, [(source, source + steps) for source in range(i...  143 us
    ppermute x40, waiting for transfers between devices, from_behind(): lax.ppermute(value, axis, [(source, source + steps) for source in range(i...  45.9 us
    unnamed x86, local copies, waits for them, and re-layouts  9.41 us
    ppermute x8, local copies, waits for them, and re-layouts, from_behind(): lax.ppermute(value, axis, [(source, source + steps) for source in range(i...  8.65 us
    dot_general x4, local copies, waits for them, and re-layouts, tile_scores(): jnp.einsum('ihd,jhd->hij', row_keys, column_keys, preferred_element_type=...  6.83 us
    dot_general x5, matrix products, tile_scores(): jnp.einsum('ihd,jhd->hij', row_keys, column_keys, preferred_element_type=...  5.58 us
  transfers between devices with their start and end apart: 41, of which 11 were waited for; matrix products, arithmetic and copies ran while one was open for 20% of the time, Pallas kernels for 0%

commit v1 on v0

v1 whole, which is shorter than its diff:
```python
import jax
import jax.numpy as jnp
from jax import lax
from jax.experimental import pallas as pl
from jax.experimental.pallas import tpu as pltpu
from jax.sharding import PartitionSpec as P

HD = 64
TOK = 256
HEADS_DEV = 4
D = 1024
RINGS = 16
RING = 8
NBLK = 128
ROWS = 3 * HD + 16
MESH = pl.DeviceIdType.MESH
START = -1e30
NEGATIVE = -1e30
BARRED = -3e30


def kernel(
    q_ref,
    v_ref,
    g_ref,
    scale_ref,
    reach_ref,
    w_ref,
    mixed_ref,
    vgrad_ref,
    send,
    buf,
    kf,
    kb,
    kta,
    top,
    tot,
    acc,
    lse,
    att,
    att_recv,
    vg,
    vg_recv,
    w_other,
    slot_sem,
    send_sem,
    lse_sem,
    lse_send_sem,
    att_sem,
    att_send_sem,
    vg_sem,
    vg_send_sem,
    w_sem,
    w_send_sem,
):
    me = lax.axis_index("seq")
    grp = lax.axis_index("head")
    ring = me // RING
    inner = me % RING
    y = inner // 2
    k = inner % 2
    other = 1 - grp
    home = y // 2
    partner = me + 1 - 2 * k
    prev_ring = ((ring + RINGS - 1) % RINGS) * RING
    next_ring = ((ring + 1) % RINGS) * RING
    up = y // 2

    halo_from = prev_ring * (1 - k) + next_ring * k + 4 * (1 - k)
    lse_peer = (prev_ring + 2 * y + 1) * (1 - k) + (next_ring + 2 * y) * k
    halo_to = (next_ring) * up + (prev_ring + 1) * (1 - up)
    halo_slot = (2 * y + k - 4) * up + (2 * y + k + 8) * (1 - up)
    own_slot = 2 * y + 4 - 3 * k
    partner_slot = 2 * y + 5 * k
    is_home = (home == k).astype(jnp.int32)

    barrier = pltpu.get_barrier_semaphore()

    def greet(seq, head):
        pl.semaphore_signal(barrier, inc=1, device_id=(seq, head), device_id_type=MESH)

    greet(partner, grp)
    for step in range(1, 4):
        greet(ring * RING + 2 * ((y + step) % 4) + k, grp)
    for j in range(4):
        greet(halo_from + j, grp)
    greet(lse_peer, grp)
    for h in range(4):
        source = ring * RING + 2 * h + home
        greet(source, other)

        @pl.when(jnp.logical_not(source == me))
        def _():
            greet(source, grp)

    greet(me, other)

    q_t = q_ref[...].T
    v_t = v_ref[...].T
    g_t = g_ref[...].T
    reach_rows = jnp.full((16, TOK), reach_ref[0].astype(jnp.float32)).astype(jnp.bfloat16)
    for h in range(HEADS_DEV):
        part = q_t[h * HD : (h + 1) * HD, :].astype(jnp.float32)
        square = jnp.sum(part * part, axis=0, keepdims=True)
        direction = part * lax.rsqrt(square + 1e-06)
        send[h, 0:HD, :] = (direction * scale_ref[h : h + 1, :]).astype(jnp.bfloat16)
        send[h, HD : 2 * HD, :] = v_t[h * HD : (h + 1) * HD, :]
        send[h, 2 * HD : 3 * HD, :] = g_t[h * HD : (h + 1) * HD, :]
        send[h, 3 * HD :, :] = reach_rows

    pl.semaphore_wait(barrier, 18 - is_home)

    def block_copy(src, slot, sent, seq):
        return pltpu.make_async_remote_copy(
            src_ref=src,
            dst_ref=buf.at[slot],
            send_sem=send_sem.at[sent],
            recv_sem=slot_sem.at[slot],
            device_id=(seq, grp),
            device_id_type=MESH,
        )

    block_copy(send.at[y], partner_slot, 0, partner).start()
    for step in (2, 1, 3):
        target = (y + step) % 4
        block_copy(send.at[target], own_slot, step, ring * RING + 2 * target + k).start()
    for h in range(4):
        block_copy(send.at[h], halo_slot, 4 + h, halo_to + 2 * h).start()
    half = pl.multiple_of(k * 128, 128)
    w_copy = pltpu.make_async_remote_copy(
        src_ref=w_ref.at[pl.ds(half, 128)],
        dst_ref=w_other.at[pl.ds(half, 128)],
        send_sem=w_send_sem.at[0],
        recv_sem=w_sem.at[0],
        device_id=(me, other),
        device_id_type=MESH,
    )
    w_copy.start()
    buf[own_slot] = send[y]

    def arrived(slot):
        block_copy(send.at[0], slot, 0, partner).wait_recv()

    for step in (1, 3, 2):
        source = (y + step) % 4
        slot = 2 * source + 4 - 3 * k
        arrived(slot)
        block_copy(buf.at[slot], 2 * source + 5 * k, 7 + step, partner).start()
    for source in range(4):
        arrived(2 * source + 5 - 5 * k)

    def turn(slot):
        kf[slot] = buf[slot, 0:HD, :].T

    def turn_ring(i, carry):
        turn(i + 4 * (1 - k))
        return carry

    lax.fori_loop(0, 8, turn_ring, 0)

    for b in range(4):
        top[b] = jnp.full((1, TOK), START, jnp.float32)
        tot[b] = jnp.zeros((1, TOK), jnp.float32)
        acc[b] = jnp.zeros((HD, TOK), jnp.float32)

    first_block = ring * RING + 4 * k - 4

    def allowed_row(slot, b, distance):
        index = first_block + slot
        valid = jnp.logical_and(index >= 0, index < NBLK)
        needed = jnp.where(valid, distance, 99).astype(jnp.float32)
        far = buf[slot, 3 * HD :, :].astype(jnp.float32)[0:1]
        own = buf[4 + b, 3 * HD :, :].astype(jnp.float32)[0:1]
        return needed <= jnp.minimum(far, own)

    def diagonal():
        return lax.broadcasted_iota(jnp.int32, (TOK, TOK), 0) == lax.broadcasted_iota(
            jnp.int32, (TOK, TOK), 1
        )

    def forward_tile(slot, b, distance, own, state):
        scores = jnp.dot(kf[slot], buf[4 + b, 0:HD, :], preferred_element_type=jnp.float32)
        if own:
            scores = jnp.where(diagonal(), NEGATIVE, scores)
        tile_top = jnp.max(scores, axis=0, keepdims=True)
        exponent = jnp.exp(scores - tile_top)
        tile_sum = jnp.sum(exponent, axis=0, keepdims=True)
        numerator = jnp.dot(
            buf[slot, HD : 2 * HD, :],
            exponent.astype(jnp.bfloat16),
            preferred_element_type=jnp.float32,
        )
        if not own:
            tile_top = jnp.where(allowed_row(slot, b, distance), tile_top, BARRED)
        old_top, old_tot, old_acc = state
        new_top = jnp.maximum(old_top, tile_top)
        keep = jnp.exp(old_top - new_top)
        add = jnp.exp(tile_top - new_top)
        return (
            new_top,
            keep * old_tot + add * tile_sum,
            keep * old_acc + add * numerator,
        )

    def load_state(b):
        return top[b], tot[b], acc[b]

    def store_state(b, state):
        top[b], tot[b], acc[b] = state

    def forward_square(i, carry):
        for step in range(4):
            b = (i + step) % 4
            gap = jnp.abs(i - b)
            store_state(b, forward_tile(4 + i, b, gap, step == 0, load_state(b)))
        return carry

    lax.fori_loop(0, 4, forward_square, 0)

    def corner(right, m, q):
        slot = (8 + m) * right + (3 - m) * (1 - right)
        b = q * right + (3 - q) * (1 - right)
        return slot, b

    def forward_side(phase, carry):
        right = jnp.where(phase == 0, 1 - k, k)

        @pl.when(phase == 1)
        def _():
            for m in range(4):
                slot, _ = corner(right, m, 0)
                arrived(slot)
                turn(slot)

        for q in range(4):
            b = q * right + (3 - q) * (1 - right)
            state = load_state(b)
            for m in range(q + 1):
                slot, _ = corner(right, m, q)
                state = forward_tile(slot, b, 4 + m - q, False, state)
            store_state(b, state)
        return carry

    lax.fori_loop(0, 2, forward_side, 0)

    denominators = [top[b] + jnp.log(tot[b]) for b in range(4)]
    lse[1] = jnp.concatenate(denominators + denominators, axis=0)
    for b in range(4):
        att[b] = (acc[b] * (1.0 / tot[b])).astype(jnp.bfloat16)

    def lse_copy(which, place, seq):
        return pltpu.make_async_remote_copy(
            src_ref=lse.at[1],
            dst_ref=lse.at[place],
            send_sem=lse_send_sem.at[which],
            recv_sem=lse_sem.at[place],
            device_id=(seq, grp),
            device_id_type=MESH,
        )

    lse_copy(0, 2 * k, partner).start()
    lse_copy(1, 2 * (1 - k), lse_peer).start()

    def att_copy(b, head):
        return pltpu.make_async_remote_copy(
            src_ref=att.at[b, :, pl.ds(pl.multiple_of(head * 128, 128), 128)],
            dst_ref=att_recv.at[grp * 4 + y],
            send_sem=att_send_sem.at[b, head],
            recv_sem=att_sem.at[grp * 4 + y],
            device_id=(ring * RING + 4 * k + b, head),
            device_id_type=MESH,
        )

    def owner(b):
        return ring * RING + 4 * k + b

    for b in range(4):
        att_copy(b, other).start()

        @pl.when(jnp.logical_not(owner(b) == me))
        def _():
            att_copy(b, grp).start()

    @pl.when(home == k)
    def _():
        b = inner - 4 * k
        att_recv[grp * 4 + y] = att[b, :, pl.ds(pl.multiple_of(grp * 128, 128), 128)]

    w_copy.wait_recv()
    pltpu.make_async_remote_copy(
        src_ref=w_other.at[pl.ds(half, 128)],
        dst_ref=w_other.at[pl.ds(half, 128)],
        send_sem=w_send_sem.at[1],
        recv_sem=w_sem.at[1],
        device_id=(partner, grp),
        device_id_type=MESH,
    ).start()

    ones = (lax.broadcasted_iota(jnp.int32, (HD, TOK), 0) < 3).astype(jnp.bfloat16)

    def turn_back(place, row):
        slot = 4 * place + row
        value = -lse[place, pl.ds(row, 1), :]
        high = value.astype(jnp.bfloat16).astype(jnp.float32)
        middle = (value - high).astype(jnp.bfloat16).astype(jnp.float32)
        low = value - high - middle
        index = lax.broadcasted_iota(jnp.int32, (HD, TOK), 0)
        extra = jnp.where(
            index == 0, high, jnp.where(index == 1, middle, jnp.where(index == 2, low, 0.0))
        ).astype(jnp.bfloat16)
        full = jnp.concatenate([buf[slot, 0:HD, :], extra], axis=0)
        kb[slot] = full.T

    for b in range(4):
        kta[b] = jnp.concatenate([buf[4 + b, 0:HD, :], ones], axis=0)
        acc[b] = jnp.zeros((HD, TOK), jnp.float32)

    for row in range(4):
        turn_back(1, row)

    def backward_tile(slot, b, distance, own):
        shifted = jnp.dot(kb[slot], kta[b], preferred_element_type=jnp.float32)
        if own:
            shifted = jnp.where(diagonal(), NEGATIVE, shifted)
        weights = jnp.exp(shifted).astype(jnp.bfloat16)
        part = jnp.dot(
            buf[slot, 2 * HD : 3 * HD, :], weights, preferred_element_type=jnp.float32
        )
        if own:
            return part
        return jnp.where(allowed_row(slot, b, distance), part, 0.0)

    def backward_square(i, carry):
        for step in range(4):
            b = (i + step) % 4
            gap = jnp.abs(i - b)
            acc[b] = acc[b] + backward_tile(4 + i, b, gap, step == 0)
        return carry

    lax.fori_loop(0, 4, backward_square, 0)

    def backward_side(phase, carry):
        right = jnp.where(phase == 0, 1 - k, k)
        place = 2 * right
        lse_copy(0, place, partner).wait_recv()
        for row in range(4):
            turn_back(place, row)
        for q in range(4):
            b = q * right + (3 - q) * (1 - right)
            total = acc[b]
            for m in range(q + 1):
                slot, _ = corner(right, m, q)
                total = total + backward_tile(slot, b, 4 + m - q, False)
            acc[b] = total
        return carry

    lax.fori_loop(0, 2, backward_side, 0)

    for b in range(4):
        vg[b] = acc[b].astype(jnp.bfloat16)

    def vg_copy(b):
        return pltpu.make_async_remote_copy(
            src_ref=vg.at[b],
            dst_ref=vg_recv.at[y],
            send_sem=vg_send_sem.at[b],
            recv_sem=vg_sem.at[y],
            device_id=(owner(b), grp),
            device_id_type=MESH,
        )

    for b in range(4):

        @pl.when(jnp.logical_not(owner(b) == me))
        def _():
            vg_copy(b).start()

    @pl.when(home == k)
    def _():
        vg_recv[y] = vg[inner - 4 * k]

    def att_arrived(place):
        pltpu.make_async_remote_copy(
            src_ref=att.at[0, :, pl.ds(0, 128)],
            dst_ref=att_recv.at[place],
            send_sem=att_send_sem.at[0, 0],
            recv_sem=att_sem.at[place],
            device_id=(me, other),
            device_id_type=MESH,
        ).wait_recv()

    for h in range(4):
        att_arrived(other * 4 + h)

        @pl.when(jnp.logical_not(ring * RING + 2 * h + home == me))
        def _():
            att_arrived(grp * 4 + h)

    pltpu.make_async_remote_copy(
        src_ref=w_other.at[pl.ds(half, 128)],
        dst_ref=w_other.at[pl.ds(half, 128)],
        send_sem=w_send_sem.at[1],
        recv_sem=w_sem.at[1],
        device_id=(partner, grp),
        device_id_type=MESH,
    ).wait_recv()
    mine = att_recv[pl.ds(grp * 4, 4)].reshape(4 * HD, 128).T
    theirs = att_recv[pl.ds(other * 4, 4)].reshape(4 * HD, 128).T
    mixed_ref[...] = (
        jnp.dot(mine, w_ref[...], preferred_element_type=jnp.float32)
        + jnp.dot(theirs, w_other[...], preferred_element_type=jnp.float32)
    ).astype(jnp.bfloat16)

    for h in range(4):

        @pl.when(jnp.logical_not(ring * RING + 2 * h + home == me))
        def _():
            pltpu.make_async_remote_copy(
                src_ref=vg.at[0],
                dst_ref=vg_recv.at[h],
                send_sem=vg_send_sem.at[0],
                recv_sem=vg_sem.at[h],
                device_id=(partner, grp),
                device_id_type=MESH,
            ).wait_recv()

    vgrad_ref[...] = vg_recv[...].reshape(4 * HD, TOK).T

    for sent in range(11):
        block_copy(send.at[0], 0, sent, partner).wait_send()
    w_copy.wait_send()
    pltpu.make_async_remote_copy(
        src_ref=w_other.at[pl.ds(half, 128)],
        dst_ref=w_other.at[pl.ds(half, 128)],
        send_sem=w_send_sem.at[1],
        recv_sem=w_sem.at[1],
        device_id=(partner, grp),
        device_id_type=MESH,
    ).wait_send()
    lse_copy(0, 0, partner).wait_send()
    lse_copy(1, 0, partner).wait_send()
    for b in range(4):
        att_copy(b, other).wait_send()

        @pl.when(jnp.logical_not(owner(b) == me))
        def _():
            att_copy(b, grp).wait_send()
            vg_copy(b).wait_send()


def shards(queries, values, scales, block_reach, out_weight, out_grad):
    vmem = pl.BlockSpec(memory_space=pltpu.VMEM)
    bf16, f32 = jnp.bfloat16, jnp.float32
    dma = pltpu.SemaphoreType.DMA
    return pl.pallas_call(
        kernel,
        out_shape=(
            jax.ShapeDtypeStruct((TOK // 2, D), bf16),
            jax.ShapeDtypeStruct((TOK, HEADS_DEV * HD), bf16),
        ),
        in_specs=[vmem, vmem, vmem, vmem, pl.BlockSpec(memory_space=pltpu.SMEM), vmem],
        out_specs=(vmem, vmem),
        scratch_shapes=[
            pltpu.VMEM((4, ROWS, TOK), bf16),
            pltpu.VMEM((12, ROWS, TOK), bf16),
            pltpu.VMEM((12, TOK, HD), bf16),
            pltpu.VMEM((12, TOK, 2 * HD), bf16),
            pltpu.VMEM((4, 2 * HD, TOK), bf16),
            pltpu.VMEM((4, 1, TOK), f32),
            pltpu.VMEM((4, 1, TOK), f32),
            pltpu.VMEM((4, HD, TOK), f32),
            pltpu.VMEM((3, 8, TOK), f32),
            pltpu.VMEM((4, HD, TOK), bf16),
            pltpu.VMEM((8, HD, TOK // 2), bf16),
            pltpu.VMEM((4, HD, TOK), bf16),
            pltpu.VMEM((4, HD, TOK), bf16),
            pltpu.VMEM((TOK, D), bf16),
            dma((12,)),
            dma((11,)),
            dma((3,)),
            dma((2,)),
            dma((8,)),
            dma((4, 2)),
            dma((4,)),
            dma((4,)),
            dma((2,)),
            dma((2,)),
        ],
        compiler_params=pltpu.CompilerParams(
            collective_id=0, has_side_effects=True, vmem_limit_bytes=48 * 1024 * 1024
        ),
    )(queries, values, out_grad, scales.T, block_reach, out_weight)


def solution(mesh):
    return jax.shard_map(
        shards,
        mesh=mesh,
        in_specs=(
            P("seq", "head"),
            P("seq", "head"),
            P("seq", "head"),
            P("seq"),
            P("head", None),
            P("seq", "head"),
        ),
        out_specs=(P(("seq", "head"), None), P("seq", "head")),
        check_vma=False,
    )
```

time: 261 us -> 56.1 us (0.21)
  the two profiles are of different devices: /device:TPU:166 before, /device:TPU:1 now
where the time goes in v1:
time: 56.1 us; the launch traced here: 55.8 us
  Pallas kernels  48.7 us (87%)
  local copies, waits for them, and re-layouts  5.79 us (10%)
  between operations  1.3 us (2%)
    pallas_call x1, Pallas kernels, shards(): pl.pallas_call(kernel, out_shape=(jax.ShapeDtypeStruct((TOK // 2, D), bf1...  48.7 us
    unnamed x12, local copies, waits for them, and re-layouts  5.79 us

profile of v1, /device:TPU:1, one launch (start us, length us, event | category | flops | bytes accessed | tf_op | source)
XLA Modules:
  0.0 55.8 jit_solution(4061864101692882191)
XLA Ops:
  1.3 0.0 copy-start
  1.3 1.0 %copy-done = bf16[256,1024]{1,0:T(8,128)(2,1)S(1)} copy-done((bf16[256,1024]{1,0:T(8,128)(2,1)S(1)}, bf16[256,1024]{1,0:T(8,128)(2,1)}, u32[]{:S(2)}) %copy-start) | copy-done | bytes 524312
  2.3 0.0 copy-start.1
  2.3 0.9 %copy-done.1 = bf16[256,256]{1,0:T(8,128)(2,1)S(1)} copy-done((bf16[256,256]{1,0:T(8,128)(2,1)S(1)}, bf16[256,256]{1,0:T(8,128)(2,1)}, u32[]{:S(2)}) %copy-start.1) | copy-done | bytes 131096
  3.2 0.0 copy-start.2
  3.2 0.9 %copy-done.2 = bf16[256,256]{1,0:T(8,128)(2,1)S(1)} copy-done((bf16[256,256]{1,0:T(8,128)(2,1)S(1)}, bf16[256,256]{1,0:T(8,128)(2,1)}, u32[]{:S(2)}) %copy-start.2) | copy-done | bytes 131096
  4.1 0.0 copy-start.3
  4.1 0.9 %copy-done.3 = bf16[256,256]{1,0:T(8,128)(2,1)S(1)} copy-done((bf16[256,256]{1,0:T(8,128)(2,1)S(1)}, bf16[256,256]{1,0:T(8,128)(2,1)}, u32[]{:S(2)}) %copy-start.3) | copy-done | bytes 131096
  5.0 0.0 copy-start.4
  5.0 0.7 %copy-done.4 = f32[256,4]{0,1:T(4,128)S(1)} copy-done((f32[256,4]{0,1:T(4,128)S(1)}, f32[256,4]{0,1:T(4,128)}, u32[]{:S(2)}) %copy-start.4) | copy-done | bytes 4120
  5.7 48.7 %shard_map.77 = (bf16[128,1024]{1,0:T(8,128)(2,1)S(1)}, bf16[256,256]{1,0:T(8,128)(2,1)S(1)}) custom-call(bf16[256,256]{1,0:T(8,128)(2,1)S(1)} %copy-done.1, bf16[256,256]{1,0:T(8,128)(2,1)S(1)} %copy-done.2, bf16[256,256]{1,0:T(8,128)(2,1)S(1)} %copy-done.3, f32[4,256]{1,0:T(4,128)S(1)} %bitcast.1, s32[1]{0:T(128)S(6)} %copy.10.reach_ref, ...), custom_call_target="tpu_custom_call" | custom-call | tf_op jit(solution)/shard_map/pallas_call | solution.py:455
  54.5 0.7 %copy.11 = bf16[128,1024]{1,0:T(8,128)(2,1)} copy(bf16[128,1024]{1,0:T(8,128)(2,1)S(1)} %get-tuple-element.4) | data formatting | bytes 524288
  55.2 0.7 %copy.12 = bf16[256,256]{1,0:T(8,128)(2,1)} copy(bf16[256,256]{1,0:T(8,128)(2,1)S(1)} %get-tuple-element.5) | data formatting | bytes 262144
Async XLA Ops:
  1.3 1.0 %copy-start = (bf16[256,1024]{1,0:T(8,128)(2,1)S(1)}, bf16[256,1024]{1,0:T(8,128)(2,1)}, u32[]{:S(2)}) copy-start(bf16[256,1024]{1,0:T(8,128)(2,1)} %w_ref.1) | copy-start | bytes 1572868
  2.3 0.9 %copy-start.1 = (bf16[256,256]{1,0:T(8,128)(2,1)S(1)}, bf16[256,256]{1,0:T(8,128)(2,1)}, u32[]{:S(2)}) copy-start(bf16[256,256]{1,0:T(8,128)(2,1)} %q_ref.1) | copy-start | bytes 393220
  3.2 0.9 %copy-start.2 = (bf16[256,256]{1,0:T(8,128)(2,1)S(1)}, bf16[256,256]{1,0:T(8,128)(2,1)}, u32[]{:S(2)}) copy-start(bf16[256,256]{1,0:T(8,128)(2,1)} %v_ref.1) | copy-start | bytes 393220
  4.1 0.9 %copy-start.3 = (bf16[256,256]{1,0:T(8,128)(2,1)S(1)}, bf16[256,256]{1,0:T(8,128)(2,1)}, u32[]{:S(2)}) copy-start(bf16[256,256]{1,0:T(8,128)(2,1)} %g_ref.1) | copy-start | bytes 393220
  5.0 0.7 %copy-start.4 = (f32[256,4]{0,1:T(4,128)S(1)}, f32[256,4]{0,1:T(4,128)}, u32[]{:S(2)}) copy-start(f32[256,4]{0,1:T(4,128)} %param.8) | copy-start | bytes 12292

commit v2 on v1

v2 whole, which is shorter than its diff:
```python
import jax
import jax.numpy as jnp
from jax import lax
from jax.experimental import pallas as pl
from jax.experimental.pallas import tpu as pltpu
from jax.sharding import PartitionSpec as P

HD = 64
TOK = 256
HEADS_DEV = 4
D = 1024
RINGS = 16
RING = 8
NBLK = 128
ROWS = 2 * HD + 16
MESH = pl.DeviceIdType.MESH
START = -1e30
NEGATIVE = -1e30
BARRED = -3e30


def kernel(
    q_hbm,
    v_hbm,
    g_hbm,
    scale_hbm,
    reach_ref,
    w_hbm,
    mixed_ref,
    vgrad_ref,
    q_ref,
    v_ref,
    g_ref,
    scale_ref,
    w_ref,
    send,
    send_g,
    buf,
    buf_g,
    kf,
    tiles,
    weights,
    columns,
    top,
    tot,
    acc,
    lse,
    att,
    att_recv,
    vg,
    vg_recv,
    w_other,
    slot_sem,
    send_sem,
    slot_g_sem,
    send_g_sem,
    lse_sem,
    lse_send_sem,
    att_sem,
    att_send_sem,
    vg_sem,
    vg_send_sem,
    w_sem,
    w_send_sem,
    in_sem,
):
    me = lax.axis_index("seq")
    grp = lax.axis_index("head")
    ring = me // RING
    inner = me % RING
    y = inner // 2
    k = inner % 2
    other = 1 - grp
    home = y // 2
    partner = me + 1 - 2 * k
    prev_ring = ((ring + RINGS - 1) % RINGS) * RING
    next_ring = ((ring + 1) % RINGS) * RING
    up = y // 2

    halo_from = prev_ring * (1 - k) + next_ring * k + 4 * (1 - k)
    lse_peer = (prev_ring + 2 * y + 1) * (1 - k) + (next_ring + 2 * y) * k
    halo_to = (next_ring) * up + (prev_ring + 1) * (1 - up)
    halo_slot = (2 * y + k - 4) * up + (2 * y + k + 8) * (1 - up)
    own_slot = 2 * y + 4 - 3 * k
    partner_slot = 2 * y + 5 * k
    is_home = (home == k).astype(jnp.int32)
    first, last = ring == 0, ring == RINGS - 1
    gets = jnp.logical_not(jnp.logical_or(jnp.logical_and(first, k == 0), jnp.logical_and(last, k == 1)))
    gives = jnp.logical_not(jnp.logical_or(jnp.logical_and(first, up == 0), jnp.logical_and(last, up == 1)))
    expected = 13 - is_home + gets.astype(jnp.int32) + 4 * gives.astype(jnp.int32)

    barrier = pltpu.get_barrier_semaphore()
    loads = [
        pltpu.make_async_copy(source, target, in_sem.at[i])
        for i, (source, target) in enumerate(
            (
                (q_hbm, q_ref),
                (scale_hbm, scale_ref),
                (v_hbm, v_ref),
                (g_hbm, g_ref),
                (w_hbm, w_ref),
            )
        )
    ]
    for load in loads:
        load.start()

    def greet(seq, head):
        pl.semaphore_signal(barrier, inc=1, device_id=(seq, head), device_id_type=MESH)

    greet(partner, grp)
    for step in range(1, 4):
        greet(ring * RING + 2 * ((y + step) % 4) + k, grp)

    @pl.when(gets)
    def _():
        for j in range(4):
            greet(halo_from + j, grp)
        greet(lse_peer, grp)

    for h in range(4):
        source = ring * RING + 2 * h + home
        greet(source, other)

        @pl.when(jnp.logical_not(source == me))
        def _():
            greet(source, grp)

    greet(me, other)

    for load in loads[:4]:
        load.wait()
    q_t = q_ref[...].T
    v_t = v_ref[...].T
    g_t = g_ref[...].T
    reach_rows = jnp.full((16, TOK), reach_ref[0].astype(jnp.float32)).astype(jnp.bfloat16)
    for h in range(HEADS_DEV):
        part = q_t[h * HD : (h + 1) * HD, :].astype(jnp.float32)
        square = jnp.sum(part * part, axis=0, keepdims=True)
        direction = part * lax.rsqrt(square + 1e-06)
        send[h, 0:HD, :] = (direction * scale_ref[h : h + 1, :]).astype(jnp.bfloat16)
        send[h, HD : 2 * HD, :] = v_t[h * HD : (h + 1) * HD, :]
        send[h, 2 * HD :, :] = reach_rows
        send_g[h] = g_t[h * HD : (h + 1) * HD, :]

    pl.semaphore_wait(barrier, expected)

    def block_copy(src, slot, sent, seq):
        return pltpu.make_async_remote_copy(
            src_ref=src,
            dst_ref=buf.at[slot],
            send_sem=send_sem.at[sent],
            recv_sem=slot_sem.at[slot],
            device_id=(seq, grp),
            device_id_type=MESH,
        )

    def grad_copy(src, slot, sent, seq):
        return pltpu.make_async_remote_copy(
            src_ref=src,
            dst_ref=buf_g.at[slot],
            send_sem=send_g_sem.at[sent],
            recv_sem=slot_g_sem.at[slot],
            device_id=(seq, grp),
            device_id_type=MESH,
        )

    for step in (2, 1, 3):
        target = (y + step) % 4
        block_copy(send.at[target], own_slot, step, ring * RING + 2 * target + k).start()
    block_copy(send.at[y], partner_slot, 0, partner).start()

    @pl.when(gives)
    def _():
        for step in (0, 1, 3, 2):
            target = (y + step) % 4
            block_copy(send.at[target], halo_slot, 4 + step, halo_to + 2 * target).start()

    for step in (2, 1, 3):
        target = (y + step) % 4
        grad_copy(send_g.at[target], own_slot, step, ring * RING + 2 * target + k).start()
    grad_copy(send_g.at[y], partner_slot, 0, partner).start()

    @pl.when(gives)
    def _():
        for step in (0, 1, 3, 2):
            target = (y + step) % 4
            grad_copy(send_g.at[target], halo_slot, 4 + step, halo_to + 2 * target).start()

    half = pl.multiple_of(k * 128, 128)
    w_copy = pltpu.make_async_remote_copy(
        src_ref=w_hbm.at[pl.ds(half, 128)],
        dst_ref=w_other.at[pl.ds(half, 128)],
        send_sem=w_send_sem.at[0],
        recv_sem=w_sem.at[0],
        device_id=(me, other),
        device_id_type=MESH,
    )
    w_copy.start()
    buf[own_slot] = send[y]
    buf_g[own_slot] = send_g[y]

    @pl.when(jnp.logical_not(gets))
    def _():
        for m in range(4):
            slot = (8 + m) * k + m * (1 - k)
            buf[slot] = jnp.zeros((ROWS, TOK), jnp.bfloat16)
            buf_g[slot] = jnp.zeros((HD, TOK), jnp.bfloat16)
        lse[2 * k] = jnp.zeros((8, TOK), jnp.float32)

    def arrived(slot):
        block_copy(send.at[0], slot, 0, partner).wait_recv()

    def grad_arrived(slot):
        grad_copy(send_g.at[0], slot, 0, partner).wait_recv()

    for step in (1, 3, 2):
        source = (y + step) % 4
        slot = 2 * source + 4 - 3 * k
        arrived(slot)
        block_copy(buf.at[slot], 2 * source + 5 * k, 7 + step, partner).start()
    for source in range(4):
        arrived(2 * source + 5 - 5 * k)

    def turn(slot):
        kf[slot] = buf[slot, 0:HD, :].T

    first_block = ring * RING + 4 * k - 4

    def allowed_row(slot, b, distance):
        index = first_block + slot
        valid = jnp.logical_and(index >= 0, index < NBLK)
        needed = jnp.where(valid, distance, 99).astype(jnp.float32)
        far = buf[slot, 2 * HD :, :].astype(jnp.float32)[0:1]
        mine = buf[4 + b, 2 * HD :, :].astype(jnp.float32)[0:1]
        return needed <= jnp.minimum(far, mine)

    def score_tile(tile):
        slot, b, place, distance = tile
        scores = jnp.dot(kf[slot], buf[4 + b, 0:HD, :], preferred_element_type=jnp.float32)
        if distance is None:
            row = lax.broadcasted_iota(jnp.int32, (TOK, TOK), 0)
            column = lax.broadcasted_iota(jnp.int32, (TOK, TOK), 1)
            scores = jnp.where(row == column, NEGATIVE, scores)
        tiles[place] = scores

    def exponent_tile(tile, spot):
        scores = tiles[tile[2]]
        tile_top = jnp.max(scores, axis=0, keepdims=True)
        exponent = jnp.exp(scores - tile_top)
        weights[spot] = exponent.astype(jnp.bfloat16)
        return tile_top, jnp.sum(exponent, axis=0, keepdims=True)

    def merge_tile(tile, spot, tile_top, tile_sum):
        slot, b, _, distance = tile
        numerator = jnp.dot(
            buf[slot, HD : 2 * HD, :], weights[spot], preferred_element_type=jnp.float32
        )
        if distance is None:
            top[b], tot[b], acc[b] = tile_top, tile_sum, numerator
            return
        tile_top = jnp.where(allowed_row(slot, b, distance), tile_top, BARRED)
        new_top = jnp.maximum(top[b], tile_top)
        keep = jnp.exp(top[b] - new_top)
        add = jnp.exp(tile_top - new_top)
        top[b] = new_top
        tot[b] = keep * tot[b] + add * tile_sum
        acc[b] = keep * acc[b] + add * numerator

    def forward(work):
        count = len(work)
        stats = [None] * count
        for t in range(count + 3):
            if 2 <= t < count + 2:
                stats[t - 2] = exponent_tile(work[t - 2], (t - 2) % 4)
            if t < count:
                score_tile(work[t])
            if t >= 3:
                merge_tile(work[t - 3], (t - 3) % 4, *stats[t - 3])

    square = [
        (4 + i, (i + step) % 4, 9 * ((i + step) % 4) + 4 + i - (i + step) % 4, abs(i - (i + step) % 4) or None)
        for step in range(4)
        for i in range(4)
    ]

    def side(right):
        work = []
        for q in range(4):
            for m in range(q + 1):
                slot = (8 + m) * right + (3 - m) * (1 - right)
                b = q * right + (3 - q) * (1 - right)
                work.append((slot, b, 9 * b + slot - b, 4 + m - q))
        return work

    near, far = 1 - k, k

    for i in range(8):
        turn(i + 4 * near)
    forward(square + side(near))
    for step in (1, 3, 2):
        source = (y + step) % 4
        slot = 2 * source + 4 - 3 * k
        grad_arrived(slot)
        grad_copy(buf_g.at[slot], 2 * source + 5 * k, 7 + step, partner).start()
    @pl.when(gets)
    def _():
        for m in range(4):
            arrived((8 + m) * far + (3 - m) * (1 - far))

    for m in range(4):
        turn((8 + m) * far + (3 - m) * (1 - far))
    forward(side(far))

    denominators = [top[b] + jnp.log(tot[b]) for b in range(4)]
    lse[1] = jnp.concatenate(denominators + denominators, axis=0)
    for b in range(4):
        att[b] = (acc[b] * (1.0 / tot[b])).astype(jnp.bfloat16)

    def lse_copy(which, place, seq):
        return pltpu.make_async_remote_copy(
            src_ref=lse.at[1],
            dst_ref=lse.at[place],
            send_sem=lse_send_sem.at[which],
            recv_sem=lse_sem.at[place],
            device_id=(seq, grp),
            device_id_type=MESH,
        )

    @pl.when(gets)
    def _():
        lse_copy(1, 2 * (1 - k), lse_peer).start()

    lse_copy(0, 2 * k, partner).start()

    def att_copy(b, head):
        return pltpu.make_async_remote_copy(
            src_ref=att.at[b, :, pl.ds(pl.multiple_of(head * 128, 128), 128)],
            dst_ref=att_recv.at[grp * 4 + y],
            send_sem=att_send_sem.at[b, head],
            recv_sem=att_sem.at[grp * 4 + y],
            device_id=(ring * RING + 4 * k + b, head),
            device_id_type=MESH,
        )

    def owner(b):
        return ring * RING + 4 * k + b

    for b in range(4):
        att_copy(b, other).start()

        @pl.when(jnp.logical_not(owner(b) == me))
        def _():
            att_copy(b, grp).start()

    @pl.when(home == k)
    def _():
        b = inner - 4 * k
        att_recv[grp * 4 + y] = att[b, :, pl.ds(pl.multiple_of(grp * 128, 128), 128)]

    def turn_lse(place):
        for row in range(4):
            value = jnp.broadcast_to(lse[place, pl.ds(row, 1), :], (128, TOK))
            columns[4 * place + row] = value.T

    def backward_tile(tile):
        slot, b, place, distance = tile
        column = columns[slot]
        shifted = tiles[place] - jnp.concatenate([column, column], axis=1)
        share = jnp.exp(shifted).astype(jnp.bfloat16)
        part = jnp.dot(buf_g[slot], share, preferred_element_type=jnp.float32)
        if distance is None:
            return part
        return jnp.where(allowed_row(slot, b, distance), part, 0.0)

    for step in range(4):
        grad_arrived(2 * step + 5 - 5 * k)
    turn_lse(1)
    for b in range(4):
        total = None
        for tile in square:
            if tile[1] == b:
                part = backward_tile(tile)
                total = part if total is None else total + part
        acc[b] = total

    def backward_side(right):
        work = side(right)
        for q in range(4):
            first = q * (q + 1) // 2
            b = work[first][1]
            total = acc[b]
            for tile in work[first : first + q + 1]:
                total = total + backward_tile(tile)
            acc[b] = total

    lse_copy(0, 2 * near, partner).wait_recv()
    turn_lse(2 * near)
    backward_side(near)
    @pl.when(gets)
    def _():
        lse_copy(0, 2 * far, partner).wait_recv()
        for m in range(4):
            grad_arrived((8 + m) * far + (3 - m) * (1 - far))

    turn_lse(2 * far)
    backward_side(far)

    for b in range(4):
        vg[b] = acc[b].astype(jnp.bfloat16)

    def vg_copy(b):
        return pltpu.make_async_remote_copy(
            src_ref=vg.at[b],
            dst_ref=vg_recv.at[y],
            send_sem=vg_send_sem.at[b],
            recv_sem=vg_sem.at[y],
            device_id=(owner(b), grp),
            device_id_type=MESH,
        )

    for b in range(4):

        @pl.when(jnp.logical_not(owner(b) == me))
        def _():
            vg_copy(b).start()

    @pl.when(home == k)
    def _():
        vg_recv[y] = vg[inner - 4 * k]

    w_copy.wait_recv()
    pltpu.make_async_remote_copy(
        src_ref=w_other.at[pl.ds(half, 128)],
        dst_ref=w_other.at[pl.ds(half, 128)],
        send_sem=w_send_sem.at[1],
        recv_sem=w_sem.at[1],
        device_id=(partner, grp),
        device_id_type=MESH,
    ).start()

    def att_arrived(place):
        pltpu.make_async_remote_copy(
            src_ref=att.at[0, :, pl.ds(0, 128)],
            dst_ref=att_recv.at[place],
            send_sem=att_send_sem.at[0, 0],
            recv_sem=att_sem.at[place],
            device_id=(me, other),
            device_id_type=MESH,
        ).wait_recv()

    for h in range(4):
        att_arrived(other * 4 + h)

        @pl.when(jnp.logical_not(ring * RING + 2 * h + home == me))
        def _():
            att_arrived(grp * 4 + h)

    pltpu.make_async_remote_copy(
        src_ref=w_other.at[pl.ds(half, 128)],
        dst_ref=w_other.at[pl.ds(half, 128)],
        send_sem=w_send_sem.at[1],
        recv_sem=w_sem.at[1],
        device_id=(partner, grp),
        device_id_type=MESH,
    ).wait_recv()
    loads[4].wait()
    mine = att_recv[pl.ds(grp * 4, 4)].reshape(4 * HD, 128).T
    theirs = att_recv[pl.ds(other * 4, 4)].reshape(4 * HD, 128).T
    mixed_ref[...] = (
        jnp.dot(mine, w_ref[...], preferred_element_type=jnp.float32)
        + jnp.dot(theirs, w_other[...], preferred_element_type=jnp.float32)
    ).astype(jnp.bfloat16)

    for h in range(4):

        @pl.when(jnp.logical_not(ring * RING + 2 * h + home == me))
        def _():
            pltpu.make_async_remote_copy(
                src_ref=vg.at[0],
                dst_ref=vg_recv.at[h],
                send_sem=vg_send_sem.at[0],
                recv_sem=vg_sem.at[h],
                device_id=(partner, grp),
                device_id_type=MESH,
            ).wait_recv()

    vgrad_ref[...] = vg_recv[...].reshape(4 * HD, TOK).T

    for sent in (0, 1, 2, 3, 8, 9, 10):
        block_copy(send.at[0], 0, sent, partner).wait_send()
        grad_copy(send_g.at[0], 0, sent, partner).wait_send()

    @pl.when(gives)
    def _():
        for sent in range(4, 8):
            block_copy(send.at[0], 0, sent, partner).wait_send()
            grad_copy(send_g.at[0], 0, sent, partner).wait_send()

    w_copy.wait_send()
    pltpu.make_async_remote_copy(
        src_ref=w_other.at[pl.ds(half, 128)],
        dst_ref=w_other.at[pl.ds(half, 128)],
        send_sem=w_send_sem.at[1],
        recv_sem=w_sem.at[1],
        device_id=(partner, grp),
        device_id_type=MESH,
    ).wait_send()
    lse_copy(0, 0, partner).wait_send()

    @pl.when(gets)
    def _():
        lse_copy(1, 0, partner).wait_send()

    for b in range(4):
        att_copy(b, other).wait_send()

        @pl.when(jnp.logical_not(owner(b) == me))
        def _():
            att_copy(b, grp).wait_send()
            vg_copy(b).wait_send()


def shards(queries, values, scales, block_reach, out_weight, out_grad):
    vmem = pl.BlockSpec(memory_space=pltpu.VMEM)
    hbm = pl.BlockSpec(memory_space=pltpu.HBM)
    bf16, f32 = jnp.bfloat16, jnp.float32
    dma = pltpu.SemaphoreType.DMA
    return pl.pallas_call(
        kernel,
        out_shape=(
            jax.ShapeDtypeStruct((TOK // 2, D), bf16),
            jax.ShapeDtypeStruct((TOK, HEADS_DEV * HD), bf16),
        ),
        in_specs=[hbm, hbm, hbm, hbm, pl.BlockSpec(memory_space=pltpu.SMEM), hbm],
        out_specs=(vmem, vmem),
        scratch_shapes=[
            pltpu.VMEM((TOK, HEADS_DEV * HD), bf16),
            pltpu.VMEM((TOK, HEADS_DEV * HD), bf16),
            pltpu.VMEM((TOK, HEADS_DEV * HD), bf16),
            pltpu.VMEM((HEADS_DEV, TOK), f32),
            pltpu.VMEM((HEADS_DEV * HD, D), bf16),
            pltpu.VMEM((4, ROWS, TOK), bf16),
            pltpu.VMEM((4, HD, TOK), bf16),
            pltpu.VMEM((12, ROWS, TOK), bf16),
            pltpu.VMEM((12, HD, TOK), bf16),
            pltpu.VMEM((12, TOK, HD), bf16),
            pltpu.VMEM((36, TOK, TOK), f32),
            pltpu.VMEM((4, TOK, TOK), bf16),
            pltpu.VMEM((12, TOK, 128), f32),
            pltpu.VMEM((4, 1, TOK), f32),
            pltpu.VMEM((4, 1, TOK), f32),
            pltpu.VMEM((4, HD, TOK), f32),
            pltpu.VMEM((3, 8, TOK), f32),
            pltpu.VMEM((4, HD, TOK), bf16),
            pltpu.VMEM((8, HD, TOK // 2), bf16),
            pltpu.VMEM((4, HD, TOK), bf16),
            pltpu.VMEM((4, HD, TOK), bf16),
            pltpu.VMEM((TOK, D), bf16),
            dma((12,)),
            dma((11,)),
            dma((12,)),
            dma((11,)),
            dma((3,)),
            dma((2,)),
            dma((8,)),
            dma((4, 2)),
            dma((4,)),
            dma((4,)),
            dma((2,)),
            dma((2,)),
            dma((5,)),
        ],
        compiler_params=pltpu.CompilerParams(
            collective_id=0, has_side_effects=True, vmem_limit_bytes=62 * 1024 * 1024
        ),
    )(queries, values, out_grad, scales.T, block_reach, out_weight)


def solution(mesh):
    return jax.shard_map(
        shards,
        mesh=mesh,
        in_specs=(
            P("seq", "head"),
            P("seq", "head"),
            P("seq", "head"),
            P("seq"),
            P("head", None),
            P("seq", "head"),
        ),
        out_specs=(P(("seq", "head"), None), P("seq", "head")),
        check_vma=False,
    )
```

time: 56.1 us -> 35 us (0.62)
  the two profiles are of different devices: /device:TPU:1 before, /device:TPU:131 now
where the time goes in v2:
time: 35 us; the launch traced here: 34.9 us
  Pallas kernels  31.2 us (89%)
  local copies, waits for them, and re-layouts  2.36 us (7%)
  between operations  1.29 us (4%)
    pallas_call x1, Pallas kernels, shards(): pl.pallas_call(kernel, out_shape=(jax.ShapeDtypeStruct((TOK // 2, D), bf1...  31.2 us
    unnamed x4, local copies, waits for them, and re-layouts  2.36 us

profile of v2, /device:TPU:131, one launch (start us, length us, event | category | flops | bytes accessed | tf_op | source)
XLA Modules:
  0.0 34.9 jit_solution(10649379024873164404)
XLA Ops:
  1.3 31.2 %shard_map.77 = (bf16[128,1024]{1,0:T(8,128)(2,1)}, bf16[256,256]{1,0:T(8,128)(2,1)}) custom-call(bf16[256,256]{1,0:T(8,128)(2,1)} %q_hbm.1, bf16[256,256]{1,0:T(8,128)(2,1)} %v_hbm.1, bf16[256,256]{1,0:T(8,128)(2,1)} %g_hbm.1, f32[4,256]{1,0:T(4,128)} %bitcast.1, s32[1]{0:T(128)S(6)} %copy.10.reach_ref, bf16[256,1024]{1,0:T(8,128)(2,1)} %w_hbm.1), custom_call_target="tpu_custom_call" | custom-call | tf_op jit(solution)/shard_map/pallas_call | solution.py:529
  32.5 0.0 copy-start
  32.5 1.7 %copy.11 = bf16[128,1024]{1,0:T(8,128)(2,1)} copy(bf16[128,1024]{1,0:T(8,128)(2,1)} %get-tuple-element.4) | data formatting | bytes 524288
  34.2 0.0 copy-done
  34.2 0.7 %copy.12 = bf16[256,256]{1,0:T(8,128)(2,1)} copy(bf16[256,256]{1,0:T(8,128)(2,1)S(1)} %copy-done) | data formatting | bytes 262144
Async XLA Ops:
  32.5 1.7 %copy-start = (bf16[256,256]{1,0:T(8,128)(2,1)S(1)}, bf16[256,256]{1,0:T(8,128)(2,1)}, u32[]{:S(2)}) copy-start(bf16[256,256]{1,0:T(8,128)(2,1)} %get-tuple-element.5) | copy-start | bytes 393220

commit v3 on v2

v3 whole, which is shorter than its diff:
```python
import jax
import jax.numpy as jnp
from jax import lax
from jax.experimental import pallas as pl
from jax.experimental.pallas import tpu as pltpu
from jax.sharding import PartitionSpec as P

HD = 64
TOK = 256
HEADS_DEV = 4
D = 1024
RINGS = 16
RING = 8
NBLK = 128
ROWS = 2 * HD + 16
HALF = TOK // 2
MESH = pl.DeviceIdType.MESH
START = -1e30
NEGATIVE = -1e30
BARRED = -3e30


def kernel(
    q_hbm,
    v_hbm,
    g_hbm,
    scale_hbm,
    reach_ref,
    w_hbm,
    mixed_ref,
    vgrad_ref,
    q_ref,
    v_ref,
    g_ref,
    scale_ref,
    w_ref,
    send,
    send_v,
    send_g,
    buf,
    buf_v,
    buf_g,
    kf,
    tiles,
    weights,
    columns,
    tile_tops,
    top,
    tot,
    acc,
    lse,
    att,
    att_recv,
    vg,
    vg_recv,
    w_other,
    slot_sem,
    send_sem,
    slot_v_sem,
    send_v_sem,
    slot_g_sem,
    send_g_sem,
    lse_sem,
    lse_send_sem,
    att_sem,
    att_send_sem,
    vg_sem,
    vg_send_sem,
    w_sem,
    w_send_sem,
    in_sem,
):
    me = lax.axis_index("seq")
    grp = lax.axis_index("head")
    ring = me // RING
    inner = me % RING
    y = inner // 2
    k = inner % 2
    other = 1 - grp
    home = y // 2
    partner = me + 1 - 2 * k
    prev_ring = ((ring + RINGS - 1) % RINGS) * RING
    next_ring = ((ring + 1) % RINGS) * RING
    up = y // 2
    across = me + RING - 2 * RING * (ring % 2)

    halo_from = prev_ring * (1 - k) + next_ring * k + 4 * (1 - k)
    lse_peer = (prev_ring + 2 * y + 1) * (1 - k) + (next_ring + 2 * y) * k
    halo_to = (next_ring) * up + (prev_ring + 1) * (1 - up)
    halo_slot = (2 * y + k - 4) * up + (2 * y + k + 8) * (1 - up)
    own_slot = 2 * y + 4 - 3 * k
    partner_slot = 2 * y + 5 * k
    is_home = (home == k).astype(jnp.int32)
    first, last = ring == 0, ring == RINGS - 1
    gets = jnp.logical_not(jnp.logical_or(jnp.logical_and(first, k == 0), jnp.logical_and(last, k == 1)))
    gives = jnp.logical_not(jnp.logical_or(jnp.logical_and(first, up == 0), jnp.logical_and(last, up == 1)))
    expected = 14 - is_home + gets.astype(jnp.int32) + 4 * gives.astype(jnp.int32)

    barrier = pltpu.get_barrier_semaphore()
    loads = [
        pltpu.make_async_copy(source, target, in_sem.at[i])
        for i, (source, target) in enumerate(
            (
                (q_hbm, q_ref),
                (scale_hbm, scale_ref),
                (v_hbm, v_ref),
                (g_hbm, g_ref),
                (w_hbm, w_ref),
            )
        )
    ]
    for load in loads:
        load.start()

    def greet(seq, head):
        pl.semaphore_signal(barrier, inc=1, device_id=(seq, head), device_id_type=MESH)

    greet(partner, grp)
    for step in range(1, 4):
        greet(ring * RING + 2 * ((y + step) % 4) + k, grp)

    @pl.when(gets)
    def _():
        for j in range(4):
            greet(halo_from + j, grp)
        greet(lse_peer, grp)

    for h in range(4):
        source = ring * RING + 2 * h + home
        greet(source, other)

        @pl.when(jnp.logical_not(source == me))
        def _():
            greet(source, grp)

    greet(me, other)
    greet(across, other)

    for load in loads[:4]:
        load.wait()
    q_t = q_ref[...].T
    v_t = v_ref[...].T
    g_t = g_ref[...].T
    reach_rows = jnp.full((16, HALF), reach_ref[0].astype(jnp.float32)).astype(jnp.bfloat16)
    for h in range(HEADS_DEV):
        part = q_t[h * HD : (h + 1) * HD, :].astype(jnp.float32)
        square = jnp.sum(part * part, axis=0, keepdims=True)
        direction = part * lax.rsqrt(square + 1e-06)
        key = (direction * scale_ref[h : h + 1, :]).astype(jnp.bfloat16)
        send[h, 0:HD, :] = key[:, 0:HALF]
        send[h, HD : 2 * HD, :] = key[:, HALF:]
        send[h, 2 * HD :, :] = reach_rows
        send_v[h] = v_t[h * HD : (h + 1) * HD, :]
        send_g[h] = g_t[h * HD : (h + 1) * HD, :]

    pl.semaphore_wait(barrier, expected)

    class Stream:
        def __init__(self, source, place, arrive, sent):
            self.source, self.place, self.arrive, self.sent = source, place, arrive, sent

        def copy(self, src, slot, which, seq):
            return pltpu.make_async_remote_copy(
                src_ref=src,
                dst_ref=self.place.at[slot],
                send_sem=self.sent.at[which],
                recv_sem=self.arrive.at[slot],
                device_id=(seq, grp),
                device_id_type=MESH,
            )

        def start(self):
            for step in (2, 1, 3):
                target = (y + step) % 4
                self.copy(
                    self.source.at[target], own_slot, step, ring * RING + 2 * target + k
                ).start()
            self.copy(self.source.at[y], partner_slot, 0, partner).start()

            @pl.when(gives)
            def _():
                for step in (0, 1, 3, 2):
                    target = (y + step) % 4
                    self.copy(
                        self.source.at[target], halo_slot, 4 + step, halo_to + 2 * target
                    ).start()

        def arrived(self, slot):
            self.copy(self.source.at[0], slot, 0, partner).wait_recv()

        def relay(self):
            for step in (1, 3, 2):
                source = (y + step) % 4
                slot = 2 * source + 4 - 3 * k
                self.arrived(slot)
                self.copy(self.place.at[slot], 2 * source + 5 * k, 7 + step, partner).start()

        def ring_arrived(self):
            for source in range(4):
                self.arrived(2 * source + 5 - 5 * k)

        def halo_arrived(self):
            @pl.when(gets)
            def _():
                for m in range(4):
                    self.arrived((8 + m) * k + (3 - m) * (1 - k))

        def finish(self):
            for which in (0, 1, 2, 3, 8, 9, 10):
                self.copy(self.source.at[0], 0, which, partner).wait_send()

            @pl.when(gives)
            def _():
                for which in range(4, 8):
                    self.copy(self.source.at[0], 0, which, partner).wait_send()

    keys = Stream(send, buf, slot_sem, send_sem)
    vals = Stream(send_v, buf_v, slot_v_sem, send_v_sem)
    grads = Stream(send_g, buf_g, slot_g_sem, send_g_sem)
    for stream in (keys, vals, grads):
        stream.start()
    buf[own_slot] = send[y]
    buf_v[own_slot] = send_v[y]
    buf_g[own_slot] = send_g[y]

    @pl.when(jnp.logical_not(gets))
    def _():
        for m in range(4):
            slot = (8 + m) * k + m * (1 - k)
            buf[slot] = jnp.zeros((ROWS, HALF), jnp.bfloat16)
            buf_v[slot] = jnp.zeros((HD, TOK), jnp.bfloat16)
            buf_g[slot] = jnp.zeros((HD, TOK), jnp.bfloat16)
        lse[2 * k] = jnp.zeros((8, TOK), jnp.float32)

    keys.relay()
    keys.ring_arrived()

    def key_of(slot):
        return jnp.concatenate([buf[slot, 0:HD, :], buf[slot, HD : 2 * HD, :]], axis=1)

    def turn(slot):
        kf[slot] = key_of(slot).T

    first_block = ring * RING + 4 * k - 4

    def allowed_row(slot, b, distance):
        index = first_block + slot
        valid = jnp.logical_and(index >= 0, index < NBLK)
        needed = jnp.where(valid, distance, 99).astype(jnp.float32)
        far = buf[slot, 2 * HD :, :].astype(jnp.float32)[0:1]
        mine = buf[4 + b, 2 * HD :, :].astype(jnp.float32)[0:1]
        row = needed <= jnp.minimum(far, mine)
        return jnp.concatenate([row, row], axis=1)

    def score_tile(tile):
        slot, b, place, distance = tile
        scores = jnp.dot(kf[slot], key_of(4 + b), preferred_element_type=jnp.float32)
        if distance is None:
            row = lax.broadcasted_iota(jnp.int32, (TOK, TOK), 0)
            column = lax.broadcasted_iota(jnp.int32, (TOK, TOK), 1)
            scores = jnp.where(row == column, NEGATIVE, scores)
        tiles[place] = scores

    def exponent_tile(tile):
        slot, b, place, distance = tile
        scores = tiles[place]
        tile_top = jnp.max(scores, axis=0, keepdims=True)
        exponent = jnp.exp(scores - tile_top)
        weights[place] = exponent.astype(jnp.bfloat16)
        tile_sum = jnp.sum(exponent, axis=0, keepdims=True)
        if distance is None:
            tile_tops[place], top[b], tot[b] = tile_top, tile_top, tile_sum
            return
        tile_top = jnp.where(allowed_row(slot, b, distance), tile_top, BARRED)
        new_top = jnp.maximum(top[b], tile_top)
        tile_tops[place] = tile_top
        tot[b] = jnp.exp(top[b] - new_top) * tot[b] + jnp.exp(tile_top - new_top) * tile_sum
        top[b] = new_top

    def exponents(work):
        for t in range(len(work) + 2):
            if t >= 2:
                exponent_tile(work[t - 2])
            if t < len(work):
                score_tile(work[t])

    def numerator_tile(tile):
        slot, b, place, _ = tile
        part = jnp.dot(buf_v[slot], weights[place], preferred_element_type=jnp.float32)
        return jnp.exp(tile_tops[place] - top[b]) * part

    square = [
        (4 + i, (i + step) % 4, 9 * ((i + step) % 4) + 4 + i - (i + step) % 4, abs(i - (i + step) % 4) or None)
        for step in range(4)
        for i in range(4)
    ]

    def side(right):
        work = []
        for q in range(4):
            for m in range(q + 1):
                slot = (8 + m) * right + (3 - m) * (1 - right)
                b = q * right + (3 - q) * (1 - right)
                work.append((slot, b, 9 * b + slot - b, 4 + m - q))
        return work

    near, far = 1 - k, k

    for i in range(8):
        turn(i + 4 * near)
    exponents(square + side(near))
    vals.relay()
    keys.halo_arrived()
    for m in range(4):
        turn((8 + m) * far + (3 - m) * (1 - far))
    exponents(side(far))

    denominators = [top[b] + jnp.log(tot[b]) for b in range(4)]
    lse[1] = jnp.concatenate(denominators + denominators, axis=0)

    def lse_copy(which, place, seq):
        return pltpu.make_async_remote_copy(
            src_ref=lse.at[1],
            dst_ref=lse.at[place],
            send_sem=lse_send_sem.at[which],
            recv_sem=lse_sem.at[place],
            device_id=(seq, grp),
            device_id_type=MESH,
        )

    @pl.when(gets)
    def _():
        lse_copy(1, 2 * (1 - k), lse_peer).start()

    lse_copy(0, 2 * k, partner).start()

    def w_copy(which, seq):
        rows = pl.ds(pl.multiple_of(k * 128 + which * 64, 64), 64)
        return pltpu.make_async_remote_copy(
            src_ref=w_hbm.at[rows],
            dst_ref=w_other.at[rows],
            send_sem=w_send_sem.at[which],
            recv_sem=w_sem.at[which],
            device_id=(seq, other),
            device_id_type=MESH,
        )

    def w_relay():
        rows = pl.ds(pl.multiple_of(k * 128, 128), 128)
        return pltpu.make_async_remote_copy(
            src_ref=w_other.at[rows],
            dst_ref=w_other.at[rows],
            send_sem=w_send_sem.at[2],
            recv_sem=w_sem.at[2],
            device_id=(partner, grp),
            device_id_type=MESH,
        )

    w_copy(0, me).start()
    w_copy(1, across).start()

    vals.ring_arrived()
    for b in range(4):
        total = None
        for tile in square:
            if tile[1] == b:
                part = numerator_tile(tile)
                total = part if total is None else total + part
        acc[b] = total

    def add_side(right, tile_of):
        work = side(right)
        for q in (3, 2, 1, 0):
            first = q * (q + 1) // 2
            b = work[first][1]
            total = acc[b]
            for tile in work[first : first + q + 1]:
                total = total + tile_of(tile)
            acc[b] = total

    add_side(near, numerator_tile)
    grads.relay()
    vals.halo_arrived()
    add_side(far, numerator_tile)
    for b in range(4):
        att[b] = (acc[b] * (1.0 / tot[b])).astype(jnp.bfloat16)

    def att_copy(b, head):
        return pltpu.make_async_remote_copy(
            src_ref=att.at[b, :, pl.ds(pl.multiple_of(head * 128, 128), 128)],
            dst_ref=att_recv.at[grp * 4 + y],
            send_sem=att_send_sem.at[b, head],
            recv_sem=att_sem.at[grp * 4 + y],
            device_id=(ring * RING + 4 * k + b, head),
            device_id_type=MESH,
        )

    def owner(b):
        return ring * RING + 4 * k + b

    for b in range(4):
        att_copy(b, other).start()

        @pl.when(jnp.logical_not(owner(b) == me))
        def _():
            att_copy(b, grp).start()

    @pl.when(home == k)
    def _():
        b = inner - 4 * k
        att_recv[grp * 4 + y] = att[b, :, pl.ds(pl.multiple_of(grp * 128, 128), 128)]

    def turn_lse(place):
        for row in range(4):
            value = jnp.broadcast_to(lse[place, pl.ds(row, 1), :], (128, TOK))
            columns[4 * place + row] = value.T

    def backward_tile(tile):
        slot, b, place, distance = tile
        column = columns[slot]
        shifted = tiles[place] - jnp.concatenate([column, column], axis=1)
        share = jnp.exp(shifted).astype(jnp.bfloat16)
        part = jnp.dot(buf_g[slot], share, preferred_element_type=jnp.float32)
        if distance is None:
            return part
        return jnp.where(allowed_row(slot, b, distance), part, 0.0)

    grads.ring_arrived()
    turn_lse(1)
    for b in range(4):
        total = None
        for tile in square:
            if tile[1] == b:
                part = backward_tile(tile)
                total = part if total is None else total + part
        acc[b] = total

    lse_copy(0, 2 * near, partner).wait_recv()
    turn_lse(2 * near)
    add_side(near, backward_tile)
    @pl.when(gets)
    def _():
        lse_copy(0, 2 * far, partner).wait_recv()

    grads.halo_arrived()
    turn_lse(2 * far)
    add_side(far, backward_tile)

    for b in range(4):
        vg[b] = acc[b].astype(jnp.bfloat16)

    def vg_copy(b):
        return pltpu.make_async_remote_copy(
            src_ref=vg.at[b],
            dst_ref=vg_recv.at[y],
            send_sem=vg_send_sem.at[b],
            recv_sem=vg_sem.at[y],
            device_id=(owner(b), grp),
            device_id_type=MESH,
        )

    for b in range(4):

        @pl.when(jnp.logical_not(owner(b) == me))
        def _():
            vg_copy(b).start()

    @pl.when(home == k)
    def _():
        vg_recv[y] = vg[inner - 4 * k]

    w_copy(0, me).wait_recv()
    w_copy(1, across).wait_recv()
    w_relay().start()

    def att_arrived(place):
        pltpu.make_async_remote_copy(
            src_ref=att.at[0, :, pl.ds(0, 128)],
            dst_ref=att_recv.at[place],
            send_sem=att_send_sem.at[0, 0],
            recv_sem=att_sem.at[place],
            device_id=(me, other),
            device_id_type=MESH,
        ).wait_recv()

    for h in range(4):
        att_arrived(other * 4 + h)

        @pl.when(jnp.logical_not(ring * RING + 2 * h + home == me))
        def _():
            att_arrived(grp * 4 + h)

    w_relay().wait_recv()
    loads[4].wait()
    mine = att_recv[pl.ds(grp * 4, 4)].reshape(4 * HD, 128).T
    theirs = att_recv[pl.ds(other * 4, 4)].reshape(4 * HD, 128).T
    mixed_ref[...] = (
        jnp.dot(mine, w_ref[...], preferred_element_type=jnp.float32)
        + jnp.dot(theirs, w_other[...], preferred_element_type=jnp.float32)
    ).astype(jnp.bfloat16)

    for h in range(4):

        @pl.when(jnp.logical_not(ring * RING + 2 * h + home == me))
        def _():
            pltpu.make_async_remote_copy(
                src_ref=vg.at[0],
                dst_ref=vg_recv.at[h],
                send_sem=vg_send_sem.at[0],
                recv_sem=vg_sem.at[h],
                device_id=(partner, grp),
                device_id_type=MESH,
            ).wait_recv()

    vgrad_ref[...] = vg_recv[...].reshape(4 * HD, TOK).T

    for stream in (keys, vals, grads):
        stream.finish()
    w_copy(0, me).wait_send()
    w_copy(1, across).wait_send()
    w_relay().wait_send()
    lse_copy(0, 0, partner).wait_send()

    @pl.when(gets)
    def _():
        lse_copy(1, 0, partner).wait_send()

    for b in range(4):
        att_copy(b, other).wait_send()

        @pl.when(jnp.logical_not(owner(b) == me))
        def _():
            att_copy(b, grp).wait_send()
            vg_copy(b).wait_send()


def shards(queries, values, scales, block_reach, out_weight, out_grad):
    vmem = pl.BlockSpec(memory_space=pltpu.VMEM)
    hbm = pl.BlockSpec(memory_space=pltpu.HBM)

    def in_hbm(array):
        return pltpu.with_memory_space_constraint(array, pltpu.HBM)

    bf16, f32 = jnp.bfloat16, jnp.float32
    dma = pltpu.SemaphoreType.DMA
    return pl.pallas_call(
        kernel,
        out_shape=(
            jax.ShapeDtypeStruct((TOK // 2, D), bf16),
            jax.ShapeDtypeStruct((TOK, HEADS_DEV * HD), bf16),
        ),
        in_specs=[hbm, hbm, hbm, hbm, pl.BlockSpec(memory_space=pltpu.SMEM), hbm],
        out_specs=(vmem, vmem),
        scratch_shapes=[
            pltpu.VMEM((TOK, HEADS_DEV * HD), bf16),
            pltpu.VMEM((TOK, HEADS_DEV * HD), bf16),
            pltpu.VMEM((TOK, HEADS_DEV * HD), bf16),
            pltpu.VMEM((HEADS_DEV, TOK), f32),
            pltpu.VMEM((HEADS_DEV * HD, D), bf16),
            pltpu.VMEM((4, ROWS, HALF), bf16),
            pltpu.VMEM((4, HD, TOK), bf16),
            pltpu.VMEM((4, HD, TOK), bf16),
            pltpu.VMEM((12, ROWS, HALF), bf16),
            pltpu.VMEM((12, HD, TOK), bf16),
            pltpu.VMEM((12, HD, TOK), bf16),
            pltpu.VMEM((12, TOK, HD), bf16),
            pltpu.VMEM((36, TOK, TOK), f32),
            pltpu.VMEM((36, TOK, TOK), bf16),
            pltpu.VMEM((12, TOK, 128), f32),
            pltpu.VMEM((36, 1, TOK), f32),
            pltpu.VMEM((4, 1, TOK), f32),
            pltpu.VMEM((4, 1, TOK), f32),
            pltpu.VMEM((4, HD, TOK), f32),
            pltpu.VMEM((3, 8, TOK), f32),
            pltpu.VMEM((4, HD, TOK), bf16),
            pltpu.VMEM((8, HD, TOK // 2), bf16),
            pltpu.VMEM((4, HD, TOK), bf16),
            pltpu.VMEM((4, HD, TOK), bf16),
            pltpu.VMEM((TOK, D), bf16),
            dma((12,)),
            dma((11,)),
            dma((12,)),
            dma((11,)),
            dma((12,)),
            dma((11,)),
            dma((3,)),
            dma((2,)),
            dma((8,)),
            dma((4, 2)),
            dma((4,)),
            dma((4,)),
            dma((3,)),
            dma((3,)),
            dma((5,)),
        ],
        compiler_params=pltpu.CompilerParams(
            collective_id=0, has_side_effects=True, vmem_limit_bytes=40 * 1024 * 1024
        ),
    )(
        in_hbm(queries),
        in_hbm(values),
        in_hbm(out_grad),
        in_hbm(scales.T),
        block_reach,
        in_hbm(out_weight),
    )


def solution(mesh):
    return jax.shard_map(
        shards,
        mesh=mesh,
        in_specs=(
            P("seq", "head"),
            P("seq", "head"),
            P("seq", "head"),
            P("seq"),
            P("head", None),
            P("seq", "head"),
        ),
        out_specs=(P(("seq", "head"), None), P("seq", "head")),
        check_vma=False,
    )
```

time: 35 us -> 30.5 us (0.87)
  the two profiles are of different devices: /device:TPU:131 before, /device:TPU:97 now
where the time goes in v3:
time: 30.5 us; the launch traced here: 30.4 us
  Pallas kernels  27.7 us (91%)
  local copies, waits for them, and re-layouts  1.36 us (4%)
  between operations  1.29 us (4%)
    pallas_call x1, Pallas kernels, shards(): pl.pallas_call(kernel, out_shape=(jax.ShapeDtypeStruct((TOK // 2, D), bf1...  27.7 us
    unnamed x2, local copies, waits for them, and re-layouts  1.36 us

profile of v3, /device:TPU:97, one launch (start us, length us, event | category | flops | bytes accessed | tf_op | source)
XLA Modules:
  0.0 30.4 jit_solution(11049273227446281166)
XLA Ops:
  1.3 27.7 %shard_map.77 = (bf16[128,1024]{1,0:T(8,128)(2,1)S(1)}, bf16[256,256]{1,0:T(8,128)(2,1)S(1)}) custom-call(bf16[256,256]{1,0:T(8,128)(2,1)} %q_hbm.1, bf16[256,256]{1,0:T(8,128)(2,1)} %v_hbm.1, bf16[256,256]{1,0:T(8,128)(2,1)} %g_hbm.1, f32[4,256]{1,0:T(4,128)} %bitcast.1, s32[1]{0:T(128)S(6)} %copy.10.reach_ref, bf16[256,1024]{1,0:T(8,128)(2,1)} %w_hbm.1), custom_call_target="tpu_custom_call" | custom-call | tf_op jit(solution)/shard_map/pallas_call | solution.py:546
  29.0 0.7 %copy.11 = bf16[128,1024]{1,0:T(8,128)(2,1)} copy(bf16[128,1024]{1,0:T(8,128)(2,1)S(1)} %get-tuple-element.4) | data formatting | bytes 524288
  29.7 0.7 %copy.12 = bf16[256,256]{1,0:T(8,128)(2,1)} copy(bf16[256,256]{1,0:T(8,128)(2,1)S(1)} %get-tuple-element.5) | data formatting | bytes 262144

commit v4 on v3

--- a/solution.py
+++ b/solution.py
@@ -310,34 +310,11 @@
         turn(i + 4 * near)
     exponents(square + side(near))
     vals.relay()
-    keys.halo_arrived()
-    for m in range(4):
-        turn((8 + m) * far + (3 - m) * (1 - far))
-    exponents(side(far))
-
-    denominators = [top[b] + jnp.log(tot[b]) for b in range(4)]
-    lse[1] = jnp.concatenate(denominators + denominators, axis=0)
-
-    def lse_copy(which, place, seq):
-        return pltpu.make_async_remote_copy(
-            src_ref=lse.at[1],
-            dst_ref=lse.at[place],
-            send_sem=lse_send_sem.at[which],
-            recv_sem=lse_sem.at[place],
-            device_id=(seq, grp),
-            device_id_type=MESH,
-        )
-
-    @pl.when(gets)
-    def _():
-        lse_copy(1, 2 * (1 - k), lse_peer).start()
-
-    lse_copy(0, 2 * k, partner).start()
-
+    loads[4].wait()
     def w_copy(which, seq):
         rows = pl.ds(pl.multiple_of(k * 128 + which * 64, 64), 64)
         return pltpu.make_async_remote_copy(
-            src_ref=w_hbm.at[rows],
+            src_ref=w_ref.at[rows],
             dst_ref=w_other.at[rows],
             send_sem=w_send_sem.at[which],
             recv_sem=w_sem.at[which],
@@ -359,6 +336,31 @@
     w_copy(0, me).start()
     w_copy(1, across).start()
 
+    keys.halo_arrived()
+    for m in range(4):
+        turn((8 + m) * far + (3 - m) * (1 - far))
+    exponents(side(far))
+
+    denominators = [top[b] + jnp.log(tot[b]) for b in range(4)]
+    lse[1] = jnp.concatenate(denominators + denominators, axis=0)
+
+    def lse_copy(which, place, seq):
+        return pltpu.make_async_remote_copy(
+            src_ref=lse.at[1],
+            dst_ref=lse.at[place],
+            send_sem=lse_send_sem.at[which],
+            recv_sem=lse_sem.at[place],
+            device_id=(seq, grp),
+            device_id_type=MESH,
+        )
+
+    @pl.when(gets)
+    def _():
+        lse_copy(1, 2 * (1 - k), lse_peer).start()
+
+    lse_copy(0, 2 * k, partner).start()
+
+    grads.relay()
     vals.ring_arrived()
     for b in range(4):
         total = None
@@ -379,7 +381,6 @@
             acc[b] = total
 
     add_side(near, numerator_tile)
-    grads.relay()
     vals.halo_arrived()
     add_side(far, numerator_tile)
     for b in range(4):
@@ -491,7 +492,6 @@
             att_arrived(grp * 4 + h)
 
     w_relay().wait_recv()
-    loads[4].wait()
     mine = att_recv[pl.ds(grp * 4, 4)].reshape(4 * HD, 128).T
     theirs = att_recv[pl.ds(other * 4, 4)].reshape(4 * HD, 128).T
     mixed_ref[...] = (
@@ -534,6 +534,17 @@
             vg_copy(b).wait_send()
 
 
+def store(mixed_vmem, vgrad_vmem, mixed_hbm, vgrad_hbm, sem):
+    copies = [
+        pltpu.make_async_copy(mixed_vmem, mixed_hbm, sem.at[0]),
+        pltpu.make_async_copy(vgrad_vmem, vgrad_hbm, sem.at[1]),
+    ]
+    for copy in copies:
+        copy.start()
+    for copy in copies:
+        copy.wait()
+
+
 def shards(queries, values, scales, block_reach, out_weight, out_grad):
     vmem = pl.BlockSpec(memory_space=pltpu.VMEM)
     hbm = pl.BlockSpec(memory_space=pltpu.HBM)
@@ -543,7 +554,7 @@
 
     bf16, f32 = jnp.bfloat16, jnp.float32
     dma = pltpu.SemaphoreType.DMA
-    return pl.pallas_call(
+    mixed, vgrad = pl.pallas_call(
         kernel,
         out_shape=(
             jax.ShapeDtypeStruct((TOK // 2, D), bf16),
@@ -604,6 +615,19 @@
         block_reach,
         in_hbm(out_weight),
     )
+    return pl.pallas_call(
+        store,
+        out_shape=(
+            jax.ShapeDtypeStruct((TOK // 2, D), bf16),
+            jax.ShapeDtypeStruct((TOK, HEADS_DEV * HD), bf16),
+        ),
+        in_specs=[vmem, vmem],
+        out_specs=(hbm, hbm),
+        scratch_shapes=[dma((2,))],
+    )(
+        pltpu.with_memory_space_constraint(mixed, pltpu.VMEM),
+        pltpu.with_memory_space_constraint(vgrad, pltpu.VMEM),
+    )
 
 
 def solution(mesh):

time: 30.5 us -> 28.7 us (0.941)
  the two profiles are of different devices: /device:TPU:97 before, /device:TPU:131 now
where the time goes in v4:
time: 28.7 us; the launch traced here: 28.4 us
  Pallas kernels  27.1 us (94%)
  between operations  1.28 us (4%)
    pallas_call x1, Pallas kernels, shards(): pl.pallas_call(kernel, out_shape=(jax.ShapeDtypeStruct((TOK // 2, D), bf1...  26.3 us
    pallas_call x1, Pallas kernels, shards(): pl.pallas_call(store, out_shape=(jax.ShapeDtypeStruct((TOK // 2, D), bf16...  0.76 us

profile of v4, /device:TPU:131, one launch (start us, length us, event | category | flops | bytes accessed | tf_op | source)
XLA Modules:
  0.0 28.4 jit_solution(6112673687527663071)
XLA Ops:
  1.3 26.3 %shard_map.77 = (bf16[128,1024]{1,0:T(8,128)(2,1)S(1)}, bf16[256,256]{1,0:T(8,128)(2,1)S(1)}) custom-call(bf16[256,256]{1,0:T(8,128)(2,1)} %q_hbm.1, bf16[256,256]{1,0:T(8,128)(2,1)} %v_hbm.1, bf16[256,256]{1,0:T(8,128)(2,1)} %g_hbm.1, f32[4,256]{1,0:T(4,128)} %bitcast.1, s32[1]{0:T(128)S(6)} %copy.8.reach_ref, bf16[256,1024]{1,0:T(8,128)(2,1)} %w_hbm.1), custom_call_target="tpu_custom_call" | custom-call | tf_op jit(solution)/shard_map/pallas_call | solution.py:557
  27.6 0.8 %shard_map.78 = (bf16[128,1024]{1,0:T(8,128)(2,1)}, bf16[256,256]{1,0:T(8,128)(2,1)}) custom-call(bf16[128,1024]{1,0:T(8,128)(2,1)S(1)} %get-tuple-element.4.mixed_vmem, bf16[256,256]{1,0:T(8,128)(2,1)S(1)} %get-tuple-element.5.vgrad_vmem), custom_call_target="tpu_custom_call" | custom-call | tf_op jit(solution)/shard_map/pallas_call | solution.py:618

commit v5 on v4

--- a/solution.py
+++ b/solution.py
@@ -188,16 +188,21 @@
         def arrived(self, slot):
             self.copy(self.source.at[0], slot, 0, partner).wait_recv()
 
-        def relay(self):
+        def relay(self, use=None):
             for step in (1, 3, 2):
                 source = (y + step) % 4
                 slot = 2 * source + 4 - 3 * k
                 self.arrived(slot)
                 self.copy(self.place.at[slot], 2 * source + 5 * k, 7 + step, partner).start()
-
-        def ring_arrived(self):
-            for source in range(4):
-                self.arrived(2 * source + 5 - 5 * k)
+                if use is not None:
+                    use(slot)
+
+        def ring_arrived(self, use=None):
+            for step in (0, 1, 3, 2):
+                slot = 2 * ((y + step) % 4) + 5 - 5 * k
+                self.arrived(slot)
+                if use is not None:
+                    use(slot)
 
         def halo_arrived(self):
             @pl.when(gets)
@@ -232,14 +237,15 @@
             buf_g[slot] = jnp.zeros((HD, TOK), jnp.bfloat16)
         lse[2 * k] = jnp.zeros((8, TOK), jnp.float32)
 
-    keys.relay()
-    keys.ring_arrived()
-
     def key_of(slot):
         return jnp.concatenate([buf[slot, 0:HD, :], buf[slot, HD : 2 * HD, :]], axis=1)
 
     def turn(slot):
         kf[slot] = key_of(slot).T
+
+    turn(own_slot)
+    keys.relay(turn)
+    keys.ring_arrived(turn)
 
     first_block = ring * RING + 4 * k - 4
 
@@ -306,36 +312,41 @@
 
     near, far = 1 - k, k
 
-    for i in range(8):
-        turn(i + 4 * near)
     exponents(square + side(near))
     vals.relay()
     loads[4].wait()
-    def w_copy(which, seq):
-        rows = pl.ds(pl.multiple_of(k * 128 + which * 64, 64), 64)
+    def w_copy(batch, which, seq):
+        rows = pl.ds(pl.multiple_of(k * 128 + batch * 64 + which * 32, 32), 32)
         return pltpu.make_async_remote_copy(
             src_ref=w_ref.at[rows],
             dst_ref=w_other.at[rows],
-            send_sem=w_send_sem.at[which],
-            recv_sem=w_sem.at[which],
+            send_sem=w_send_sem.at[2 * batch + which],
+            recv_sem=w_sem.at[2 * batch + which],
             device_id=(seq, other),
             device_id_type=MESH,
         )
 
-    def w_relay():
-        rows = pl.ds(pl.multiple_of(k * 128, 128), 128)
+    def w_relay(batch):
+        rows = pl.ds(pl.multiple_of(k * 128 + batch * 64, 64), 64)
         return pltpu.make_async_remote_copy(
             src_ref=w_other.at[rows],
             dst_ref=w_other.at[rows],
-            send_sem=w_send_sem.at[2],
-            recv_sem=w_sem.at[2],
+            send_sem=w_send_sem.at[4 + batch],
+            recv_sem=w_sem.at[4 + batch],
             device_id=(partner, grp),
             device_id_type=MESH,
         )
 
-    w_copy(0, me).start()
-    w_copy(1, across).start()
-
+    def send_w(batch):
+        w_copy(batch, 0, me).start()
+        w_copy(batch, 1, across).start()
+
+    def pass_w(batch):
+        w_copy(batch, 0, me).wait_recv()
+        w_copy(batch, 1, across).wait_recv()
+        w_relay(batch).start()
+
+    send_w(0)
     keys.halo_arrived()
     for m in range(4):
         turn((8 + m) * far + (3 - m) * (1 - far))
@@ -359,6 +370,7 @@
         lse_copy(1, 2 * (1 - k), lse_peer).start()
 
     lse_copy(0, 2 * k, partner).start()
+    send_w(1)
 
     grads.relay()
     vals.ring_arrived()
@@ -470,9 +482,8 @@
     def _():
         vg_recv[y] = vg[inner - 4 * k]
 
-    w_copy(0, me).wait_recv()
-    w_copy(1, across).wait_recv()
-    w_relay().start()
+    pass_w(0)
+    pass_w(1)
 
     def att_arrived(place):
         pltpu.make_async_remote_copy(
@@ -491,7 +502,8 @@
         def _():
             att_arrived(grp * 4 + h)
 
-    w_relay().wait_recv()
+    w_relay(0).wait_recv()
+    w_relay(1).wait_recv()
     mine = att_recv[pl.ds(grp * 4, 4)].reshape(4 * HD, 128).T
     theirs = att_recv[pl.ds(other * 4, 4)].reshape(4 * HD, 128).T
     mixed_ref[...] = (
@@ -516,9 +528,10 @@
 
     for stream in (keys, vals, grads):
         stream.finish()
-    w_copy(0, me).wait_send()
-    w_copy(1, across).wait_send()
-    w_relay().wait_send()
+    for batch in range(2):
+        w_copy(batch, 0, me).wait_send()
+        w_copy(batch, 1, across).wait_send()
+        w_relay(batch).wait_send()
     lse_copy(0, 0, partner).wait_send()
 
     @pl.when(gets)
@@ -600,8 +613,8 @@
             dma((4, 2)),
             dma((4,)),
             dma((4,)),
-            dma((3,)),
-            dma((3,)),
+            dma((6,)),
+            dma((6,)),
             dma((5,)),
         ],
         compiler_params=pltpu.CompilerParams(

time: 28.7 us -> 28.5 us (level)
  no operation moved by 1% of the time
where the time goes in v5:
time: 28.5 us; the launch traced here: 28.3 us
  Pallas kernels  27 us (95%)
  between operations  1.28 us (4%)
    pallas_call x1, Pallas kernels, shards(): pl.pallas_call(kernel, out_shape=(jax.ShapeDtypeStruct((TOK // 2, D), bf1...  26.2 us
    pallas_call x1, Pallas kernels, shards(): pl.pallas_call(store, out_shape=(jax.ShapeDtypeStruct((TOK // 2, D), bf16...  0.76 us

profile of v5, /device:TPU:131, one launch (start us, length us, event | category | flops | bytes accessed | tf_op | source)
XLA Modules:
  0.0 28.3 jit_solution(16528152703040629751)
XLA Ops:
  1.3 26.2 %shard_map.77 = (bf16[128,1024]{1,0:T(8,128)(2,1)S(1)}, bf16[256,256]{1,0:T(8,128)(2,1)S(1)}) custom-call(bf16[256,256]{1,0:T(8,128)(2,1)} %q_hbm.1, bf16[256,256]{1,0:T(8,128)(2,1)} %v_hbm.1, bf16[256,256]{1,0:T(8,128)(2,1)} %g_hbm.1, f32[4,256]{1,0:T(4,128)} %bitcast.1, s32[1]{0:T(128)S(6)} %copy.8.reach_ref, bf16[256,1024]{1,0:T(8,128)(2,1)} %w_hbm.1), custom_call_target="tpu_custom_call" | custom-call | tf_op jit(solution)/shard_map/pallas_call | solution.py:570
  27.5 0.8 %shard_map.78 = (bf16[128,1024]{1,0:T(8,128)(2,1)}, bf16[256,256]{1,0:T(8,128)(2,1)}) custom-call(bf16[128,1024]{1,0:T(8,128)(2,1)S(1)} %get-tuple-element.4.mixed_vmem, bf16[256,256]{1,0:T(8,128)(2,1)S(1)} %get-tuple-element.5.vgrad_vmem), custom_call_target="tpu_custom_call" | custom-call | tf_op jit(solution)/shard_map/pallas_call | solution.py:631

commit v6 on v5

--- a/solution.py
+++ b/solution.py
@@ -136,11 +136,9 @@
     greet(me, other)
     greet(across, other)
 
-    for load in loads[:4]:
+    for load in loads[:2]:
         load.wait()
     q_t = q_ref[...].T
-    v_t = v_ref[...].T
-    g_t = g_ref[...].T
     reach_rows = jnp.full((16, HALF), reach_ref[0].astype(jnp.float32)).astype(jnp.bfloat16)
     for h in range(HEADS_DEV):
         part = q_t[h * HD : (h + 1) * HD, :].astype(jnp.float32)
@@ -150,8 +148,6 @@
         send[h, 0:HD, :] = key[:, 0:HALF]
         send[h, HD : 2 * HD, :] = key[:, HALF:]
         send[h, 2 * HD :, :] = reach_rows
-        send_v[h] = v_t[h * HD : (h + 1) * HD, :]
-        send_g[h] = g_t[h * HD : (h + 1) * HD, :]
 
     pl.semaphore_wait(barrier, expected)
 
@@ -222,8 +218,14 @@
     keys = Stream(send, buf, slot_sem, send_sem)
     vals = Stream(send_v, buf_v, slot_v_sem, send_v_sem)
     grads = Stream(send_g, buf_g, slot_g_sem, send_g_sem)
-    for stream in (keys, vals, grads):
-        stream.start()
+    keys.start()
+    for load in loads[2:4]:
+        load.wait()
+    v_t = v_ref[...].T
+    g_t = g_ref[...].T
+    for h in range(HEADS_DEV):
+        send_v[h] = v_t[h * HD : (h + 1) * HD, :]
+        send_g[h] = g_t[h * HD : (h + 1) * HD, :]
     buf[own_slot] = send[y]
     buf_v[own_slot] = send_v[y]
     buf_g[own_slot] = send_g[y]
@@ -236,6 +238,9 @@
             buf_v[slot] = jnp.zeros((HD, TOK), jnp.bfloat16)
             buf_g[slot] = jnp.zeros((HD, TOK), jnp.bfloat16)
         lse[2 * k] = jnp.zeros((8, TOK), jnp.float32)
+
+    vals.start()
+    grads.start()
 
     def key_of(slot):
         return jnp.concatenate([buf[slot, 0:HD, :], buf[slot, HD : 2 * HD, :]], axis=1)

time: 28.5 us -> 28.5 us (level)
  no operation moved by 1% of the time
where the time goes in v6:
time: 28.5 us; the launch traced here: 28.3 us
  Pallas kernels  27 us (95%)
  between operations  1.28 us (4%)
    pallas_call x1, Pallas kernels, shards(): pl.pallas_call(kernel, out_shape=(jax.ShapeDtypeStruct((TOK // 2, D), bf1...  26.2 us
    pallas_call x1, Pallas kernels, shards(): pl.pallas_call(store, out_shape=(jax.ShapeDtypeStruct((TOK // 2, D), bf16...  0.76 us

profile of v6, /device:TPU:131, one launch (start us, length us, event | category | flops | bytes accessed | tf_op | source)
XLA Modules:
  0.0 28.3 jit_solution(6426950787858518845)
XLA Ops:
  1.3 26.2 %shard_map.77 = (bf16[128,1024]{1,0:T(8,128)(2,1)S(1)}, bf16[256,256]{1,0:T(8,128)(2,1)S(1)}) custom-call(bf16[256,256]{1,0:T(8,128)(2,1)} %q_hbm.1, bf16[256,256]{1,0:T(8,128)(2,1)} %v_hbm.1, bf16[256,256]{1,0:T(8,128)(2,1)} %g_hbm.1, f32[4,256]{1,0:T(4,128)} %bitcast.1, s32[1]{0:T(128)S(6)} %copy.8.reach_ref, bf16[256,1024]{1,0:T(8,128)(2,1)} %w_hbm.1), custom_call_target="tpu_custom_call" | custom-call | tf_op jit(solution)/shard_map/pallas_call | solution.py:575
  27.5 0.8 %shard_map.78 = (bf16[128,1024]{1,0:T(8,128)(2,1)}, bf16[256,256]{1,0:T(8,128)(2,1)}) custom-call(bf16[128,1024]{1,0:T(8,128)(2,1)S(1)} %get-tuple-element.4.mixed_vmem, bf16[256,256]{1,0:T(8,128)(2,1)S(1)} %get-tuple-element.5.vgrad_vmem), custom_call_target="tpu_custom_call" | custom-call | tf_op jit(solution)/shard_map/pallas_call | solution.py:636
